TPU v7x, 32 devices: a whole 2x2x4 slice. The times are simulated.
32 devices in a mesh: rep: 8 (over z, y), shard: 4 (over x, core).
Axes of the slice: x: 2, y: 2, z: 4, core: 2. Of those that a mesh axis runs over, the one named last changes fastest.
Arguments:
- prompt: bfloat16 [8, 1024, 768], P('rep', 'shard'), may hold values from -6 to 6
- conts: bfloat16 [8, 4, 512, 768], P('rep', 'shard'), may hold values from -6 to 6
- prompt_cot: bfloat16 [8, 1024, 768], P('rep', 'shard'), may hold values from -6 to 6
- cont_cot: bfloat16 [8, 4, 512, 768], P('rep', 'shard'), may hold values from -6 to 6
- labels: int32 [8, 4], P('rep', 'shard'), may hold values from 0 to 13
- w_qkv: float32 [768, 2304], P('shard'), may hold values from -0.21875 to 0.21875
- w_out: float32 [768, 768], P('shard'), may hold values from -3.5 to 3.5
- w_in: float32 [768, 3072], P('shard'), may hold values from -0.21875 to 0.21875
- w_ffo: float32 [3072, 768], P('shard'), may hold values from -0.109375 to 0.109375
- layer_biases: float32 [6, 768], replicated, may hold values from -3 to 3
- norm_gains: float32 [2, 768], replicated, may hold values from 0.25 to 1.75
- bias_in: float32 [3072], replicated, may hold values from -3 to 3
- w_student: float32 [768, 128], replicated, may hold values from -0.21875 to 0.21875
- student_vectors: float32 [3, 128], replicated, may hold values from -4 to 4
- w_pool: float32 [128, 128], replicated, may hold values from -0.5 to 0.5
- w_class: float32 [128, 14], replicated, may hold values from -1 to 1
- bias_class: float32 [14], replicated, may hold values from -3 to 3
Outputs:
- prompt_out: bfloat16 [8, 1024, 768], P('rep', 'shard')
- cont_out: bfloat16 [8, 4, 512, 768], P('rep', 'shard')
- logits: float32 [8, 4, 14], P('rep', 'shard')
- prompt_grad: float32 [8, 1024, 768], P('rep', 'shard')
- cont_grad: float32 [8, 4, 512, 768], P('rep', 'shard')
- grad_qkv: float32 [768, 2304], P('shard')
- grad_out: float32 [768, 768], P('shard')
- grad_in: float32 [768, 3072], P('shard')
- grad_ffo: float32 [3072, 768], P('shard')
- grad_biases: float32 [6, 768], replicated
- grad_gains: float32 [2, 768], replicated
- grad_bias_in: float32 [3072], replicated
- grad_student: float32 [768, 128], replicated
- grad_student_vectors: float32 [3, 128], replicated
- grad_pool: float32 [128, 128], replicated
- grad_class: float32 [128, 14], replicated
- grad_bias_class: float32 [14], replicated
All inputs are finite; a program needn't handle non-finite values.
Results may differ from a plain program's by a relative error of at most 0.02.
Values may be sent and summed in bfloat16 or wider, within the bound.
A program may use at most 192 MiB of HBM per device.

v0:
```python
import jax
import jax.numpy as jnp
from jax import lax
from jax.experimental import pallas as pl
from jax.experimental.pallas import tpu as pltpu
from jax.sharding import PartitionSpec as P

D = 768
HEADS = 12
DH = 64
STU = 128
SHEADS = 2


HIGHEST = lax.Precision.HIGHEST
NEG_BIG = -1e30


def dot_plain(left, right):
    return jnp.dot(left, right, preferred_element_type=jnp.float32)


def dot_first(left, right):
    return lax.dot_general(
        left, right, (((0,), (0,)), ((), ())), preferred_element_type=jnp.float32
    )


def dot_second(left, right):
    return lax.dot_general(
        left, right, (((1,), (1,)), ((), ())), preferred_element_type=jnp.float32
    )


TILE = 256
PAIR = 128
VMEM_ALL = 62 * 1024 * 1024


def rows_dot(left, right):
    return lax.dot_general(
        left, right, (((1,), (1,)), ((), ())), preferred_element_type=jnp.float32
    )


def low_lanes(shape):
    return lax.broadcasted_iota(jnp.int32, shape, len(shape) - 1) < DH


def attend_fwd_pair(
    shard, prompt_rows, q, kp, vp, kc, vc, att_ref, lse_ref, between=None
):
    cont_len = kc.shape[0]
    prompt_len = kp.shape[0]
    for start in range(0, prompt_rows + cont_len, TILE):
        q_t = q[start : start + TILE, :] * jnp.asarray(DH ** (-0.5), jnp.bfloat16)
        halves = []
        for parity in range(2):
            keep = low_lanes(q_t.shape) == (parity == 0)
            q_h = jnp.where(keep, q_t, jnp.zeros_like(q_t))
            s_p = rows_dot(q_h, kp[...])
            if start < prompt_rows:
                key = lax.broadcasted_iota(jnp.int32, s_p.shape, 1)
                row = lax.broadcasted_iota(jnp.int32, s_p.shape, 0)
                s_p = jnp.where(key <= row + (shard * prompt_rows + start), s_p, NEG_BIG)
                largest = jnp.max(s_p, 1, keepdims=True)
                p_p = jnp.exp(s_p - largest)
                total = jnp.sum(p_p, 1, keepdims=True)
                o = dot_plain(p_p.astype(jnp.bfloat16), vp[...])
            else:
                seen = start - prompt_rows + TILE
                s_c = rows_dot(q_h, kc[:seen, :])
                key = lax.broadcasted_iota(jnp.int32, s_c.shape, 1)
                row = lax.broadcasted_iota(jnp.int32, s_c.shape, 0)
                s_c = jnp.where(key <= row + (start - prompt_rows), s_c, NEG_BIG)
                largest = jnp.maximum(
                    jnp.max(s_p, 1, keepdims=True), jnp.max(s_c, 1, keepdims=True)
                )
                p_p = jnp.exp(s_p - largest)
                p_c = jnp.exp(s_c - largest)
                total = jnp.sum(p_p, 1, keepdims=True) + jnp.sum(p_c, 1, keepdims=True)
                o = dot_plain(p_p.astype(jnp.bfloat16), vp[...]) + dot_plain(
                    p_c.astype(jnp.bfloat16), vc[:seen, :]
                )
            halves.append((o / total, largest + jnp.log(total)))
        keep = low_lanes((TILE, PAIR))
        att_ref[start : start + TILE, :] = jnp.where(keep, halves[0][0], halves[1][0])
        lse = jnp.where(
            keep,
            jnp.broadcast_to(halves[0][1], (TILE, PAIR)),
            jnp.broadcast_to(halves[1][1], (TILE, PAIR)),
        )
        turned = jnp.transpose(lse)
        lse_ref[0:1, start : start + TILE] = turned[0:1, :]
        lse_ref[1:2, start : start + TILE] = turned[DH : DH + 1, :]
        if between is not None:
            between(start // TILE)


def attend_bwd_pair(
    shard, prompt_rows, q, kp, vp, kc, vc, g, att, lse, dq, dkp, dvp, dkc, dvc, accum, between=None
):
    cont_len = kc.shape[0]
    tokens = prompt_rows + cont_len
    prompt_len = kp.shape[0]
    g_t = g[...]
    turned = jnp.transpose(g_t.astype(jnp.float32) * att[...])
    delta = (
        jnp.sum(turned[:DH], 0, keepdims=True),
        jnp.sum(turned[DH:], 0, keepdims=True),
    )
    q_t = q[...] * jnp.asarray(DH ** (-0.5), jnp.bfloat16)
    keep = low_lanes(q_t.shape)
    zero = jnp.zeros_like(q_t)
    q_h = (jnp.where(keep, q_t, zero), jnp.where(keep, zero, q_t))
    g_h = (jnp.where(keep, g_t, zero), jnp.where(keep, zero, g_t))
    accum[...] = jnp.zeros_like(accum)

    def block(key_b, value_b, first, mask):
        key_t = jnp.transpose(key_b.astype(jnp.float32)).astype(jnp.bfloat16)
        g_key = jnp.zeros((TILE, PAIR), jnp.float32)
        g_value = jnp.zeros((TILE, PAIR), jnp.float32)
        for parity in range(2):
            scores = rows_dot(key_b, q_h[parity][first:])
            probs = jnp.exp(scores - lse[parity : parity + 1, first:])
            masked = jnp.where(mask, probs[:, :TILE], 0.0)
            if tokens - first > TILE:
                probs = jnp.concatenate([masked, probs[:, TILE:]], 1)
            else:
                probs = masked
            g_probs = rows_dot(value_b, g_h[parity][first:])
            g_scores = (probs * (g_probs - delta[parity][:, first:])).astype(jnp.bfloat16)
            g_value += dot_plain(probs.astype(jnp.bfloat16), g_h[parity][first:])
            g_key += dot_plain(g_scores, q_h[parity][first:])
            rows = slice(parity * DH, (parity + 1) * DH)
            accum[rows, first:] += dot_plain(key_t[rows], g_scores)
        return g_key.astype(jnp.bfloat16), g_value.astype(jnp.bfloat16)

    ahead = lax.broadcasted_iota(jnp.int32, (TILE, TILE), 0) - lax.broadcasted_iota(
        jnp.int32, (TILE, TILE), 1
    )

    def prompt_block(index, start):
        rows = pl.ds(start, TILE)
        mask = ahead <= shard * prompt_rows - index * TILE
        g_key, g_value = block(kp[rows, :], vp[rows, :], 0, mask)
        dkp[rows, :] = g_key
        dvp[rows, :] = g_value

    blocks = prompt_len // TILE
    if blocks <= 4:
        for index in range(blocks):
            prompt_block(index, index * TILE)
            if between is not None:
                between(index)
    else:

        def step(index, carry):
            prompt_block(index, pl.multiple_of(index * TILE, TILE))
            return carry

        lax.fori_loop(0, blocks, step, 0)
    for start in range(0, cont_len, TILE):
        rows = slice(start, start + TILE)
        g_key, g_value = block(kc[rows, :], vc[rows, :], prompt_rows + start, ahead <= 0)
        dkc[rows, :] = g_key
        dvc[rows, :] = g_value
        if between is not None:
            between(blocks + start // TILE)
    dq[...] = (jnp.transpose(accum[...]) * DH ** (-0.5)).astype(jnp.bfloat16)


def attend_forward(q, kp, vp, kc, vc, prompt_rows):
    tokens, prompt_len, cont_len = q.shape[0], kp.shape[0], kc.shape[0]
    pairs = HEADS // 2

    def kernel(q, kp, vp, kc, vc, att_ref, lse_ref):
        attend_fwd_pair(
            lax.axis_index("shard"), prompt_rows, q, kp, vp, kc, vc, att_ref, lse_ref.at[0]
        )

    def columns(rows):
        return pl.BlockSpec((rows, PAIR), lambda p: (0, p))

    return pl.pallas_call(
        kernel,
        grid=(pairs,),
        in_specs=[columns(rows) for rows in (tokens, prompt_len, prompt_len, cont_len, cont_len)],
        out_specs=[columns(tokens), pl.BlockSpec((1, 8, tokens), lambda p: (p, 0, 0))],
        out_shape=[
            jax.ShapeDtypeStruct((tokens, D), jnp.float32),
            jax.ShapeDtypeStruct((pairs, 8, tokens), jnp.float32),
        ],
        compiler_params=pltpu.CompilerParams(vmem_limit_bytes=VMEM_ALL),
        name="attend_forward",
    )(q, kp, vp, kc, vc)


def attend_backward(q, kp, vp, kc, vc, g_att, att, lse, prompt_rows):
    tokens, prompt_len, cont_len = q.shape[0], kp.shape[0], kc.shape[0]
    pairs = HEADS // 2

    def kernel(q, kp, vp, kc, vc, g, a, ls, dq, dkp, dvp, dkc, dvc, accum):
        attend_bwd_pair(
            lax.axis_index("shard"),
            prompt_rows,
            q,
            kp,
            vp,
            kc,
            vc,
            g,
            a,
            ls.at[0],
            dq,
            dkp,
            dvp,
            dkc,
            dvc,
            accum,
        )

    def columns(rows):
        return pl.BlockSpec((rows, PAIR), lambda p: (0, p))

    sizes = (tokens, prompt_len, prompt_len, cont_len, cont_len)
    return pl.pallas_call(
        kernel,
        grid=(pairs,),
        in_specs=[columns(rows) for rows in sizes + (tokens, tokens)]
        + [pl.BlockSpec((1, 8, tokens), lambda p: (p, 0, 0))],
        out_specs=[columns(rows) for rows in sizes],
        out_shape=[jax.ShapeDtypeStruct((rows, D), jnp.bfloat16) for rows in sizes],
        scratch_shapes=[pltpu.VMEM((PAIR, tokens), jnp.float32)],
        compiler_params=pltpu.CompilerParams(vmem_limit_bytes=VMEM_ALL),
        name="attend_backward",
    )(q, kp, vp, kc, vc, g_att, att, lse)


MESH_ID = pl.DeviceIdType.MESH


def project_and_attend(prompt, conts, w_qkv, w_out, w_in, w_ffo, layer_biases):
    pieces, early = 11, 4
    by_z = (4, 5, 6, 7, 8, 9)
    rows = w_qkv.shape[0]
    p_rows, cont_len = prompt.shape[0], conts.shape[0]
    tokens = p_rows + cont_len
    p_len = 4 * p_rows
    pairs = HEADS // 2
    tiles = tokens // TILE
    chunk = 2 * PAIR
    chunks = D // chunk
    quarter = rows // 4

    def kernel(
        xp, xc, wq, wo, wi, wf, bias, w_all_out, wf_out, q_out, kc_out, vc_out, kp_out, vp_out, att_out, lse,
        stage, w_all, q, kc, vc, kp, vp, att,
        load, c_s, c_r, x_s, x_r, y_s, y_r, z_s, z_r, d_s, d_r, e_s, e_r, w_sem,
        kc_s, kc_r, kx_s, kx_r, kd_s, kd_r, out_sem,
    ):
        rep, shard = lax.axis_index("rep"), lax.axis_index("shard")
        z, y = rep // 2, rep % 2
        x, core = shard // 2, shard % 2
        partner = (rep, 2 * x + 1 - core)
        across = (rep, 2 * (1 - x) + core)
        beside = (2 * z + 1 - y, shard)
        z_low = z % 2
        above = (2 * (z + 1 - 2 * z_low) + y, shard)
        there = 2 * (1 - x) + core

        def remote(ref, send, recv, device):
            return pltpu.make_async_remote_copy(
                src_ref=ref,
                dst_ref=ref,
                send_sem=send,
                recv_sem=recv,
                device_id=device,
                device_id_type=MESH_ID,
            )

        def source(k):
            if k < 3:
                j = (1, 2, 0)[k]
                return wq.at[:, j * D : (j + 1) * D]
            if k < 4:
                return wo
            if k < 8:
                return wi.at[:, (k - 4) * D : (k - 3) * D]
            return wf.at[(k - 8) * rows : (k - 7) * rows, :]

        def loading(k):
            return pltpu.make_async_copy(source(k), stage.at[k], load.at[k])

        for k in range(pieces):
            loading(k).start()
        barrier = pltpu.get_barrier_semaphore()
        for other in (partner, across, beside, above):
            pl.semaphore_signal(barrier, inc=1, device_id=other, device_id_type=MESH_ID)
        pl.semaphore_wait(barrier, 4)

        def part(k, block, first, count):
            start = pl.multiple_of(first * quarter, 16)
            return w_all.at[k, block, pl.ds(start, count * quarter), :]

        def core_copy(k):
            return remote(w_all.at[k, shard], c_s.at[k], c_r.at[k], partner)

        def core_arrival(k):
            return remote(w_all.at[k, 2 * x + 1 - core], c_s.at[k], c_r.at[k], partner)

        def crossing(k, y_at):
            return (2 * z_low + y_at, 1) if k in by_z else (2 * y_at, 2)

        def x_copy(k):
            return remote(part(k, shard, *crossing(k, y)), x_s.at[k], x_r.at[k], across)

        def x_arrival(k):
            return remote(part(k, there, *crossing(k, y)), x_s.at[k], x_r.at[k], across)

        def y_copy(k):
            return remote(part(k, there, *crossing(k, y)), y_s.at[k], y_r.at[k], beside)

        def y_arrival(k):
            return remote(part(k, there, *crossing(k, 1 - y)), y_s.at[k], y_r.at[k], beside)

        def z_copy(k):
            return remote(part(k, there, 2 * z_low, 2), z_s.at[k], z_r.at[k], above)

        def z_arrival(k):
            return remote(part(k, there, 2 * (1 - z_low), 2), z_s.at[k], z_r.at[k], above)

        def halves(k):
            first = 2 * z_low if k in by_z else 2 * y
            return first, 2 - first

        def d_copy(k, block=None):
            block = there if block is None else block
            return remote(part(k, block, halves(k)[0], 2), d_s.at[k], d_r.at[k], partner)

        def e_copy(k, block=None):
            block = there if block is None else block
            return remote(part(k, block, halves(k)[1], 2), e_s.at[k], e_r.at[k], partner)

        far = 2 * (1 - x) + 1 - core

        def send_piece(k):
            x_copy(k).start()
            core_copy(k).start()

        def round_piece(k):
            loading(k).wait()
            w_all[k, shard] = stage[k].astype(jnp.bfloat16)

        def serve_x(k):
            x_arrival(k).wait_recv()
            y_copy(k).start()
            if k not in by_z:
                d_copy(k).start()

        def serve_y(k):
            y_arrival(k).wait_recv()
            if k in by_z:
                z_copy(k).start()
                d_copy(k).start()
            else:
                e_copy(k).start()

        def serve_z(k):
            z_arrival(k).wait_recv()
            e_copy(k).start()

        def w_store(k):
            if k < 8:
                return pltpu.make_async_copy(w_all.at[k], w_all_out.at[k], w_sem.at[k])
            return pltpu.make_async_copy(w_all.at[k], wf_out.at[:, k - 8], w_sem.at[k])

        def complete(k):
            core_arrival(k).wait_recv()
            d_copy(k, far).wait_recv()
            e_copy(k, far).wait_recv()
            w_store(k).start()

        def weight(k):
            return w_all[k].reshape(4 * rows, D)

        for k in range(early):
            round_piece(k)
            send_piece(k)
        for k in range(early, pieces):
            round_piece(k)
        own_rows = pl.ds(pl.multiple_of(shard * p_rows, p_rows), p_rows)
        kv = (kp, vp)

        def kv_part(t, g, block):
            lanes = pl.ds(g * chunk if isinstance(g, int) else pl.multiple_of(g * chunk, chunk), chunk)
            return kv[t].at[pl.ds(pl.multiple_of(block * p_rows, p_rows), p_rows), lanes]

        def kv_core(t, g):
            return remote(kv_part(t, g, shard), kc_s.at[g, t], kc_r.at[g, t], partner)

        def kv_across(t, g):
            return remote(kv_part(t, g, shard), kx_s.at[g, t], kx_r.at[g, t], across)

        def kv_forward(t, g):
            return remote(kv_part(t, g, there), kd_s.at[g, t], kd_r.at[g, t], partner)

        serve_x(0)
        serve_x(1)
        serve_y(0)
        complete(0)
        kp[own_rows, :] = dot_plain(xp[...], weight(0)).astype(jnp.bfloat16)
        kc[...] = dot_plain(xc[...], weight(0)).astype(jnp.bfloat16)
        serve_x(2)
        serve_y(1)
        complete(1)
        vp[own_rows, :] = (dot_plain(xp[...], weight(1)) + bias[1:2, :]).astype(jnp.bfloat16)
        waiting = list(range(early, pieces))
        for g in range(chunks):
            for t in range(2):
                kv_across(t, g).start()
                kv_core(t, g).start()
            for k in waiting[: 2 if g < chunks - 1 else pieces]:
                send_piece(k)
            waiting = waiting[2:]
        vc[...] = (dot_plain(xc[...], weight(1)) + bias[1:2, :]).astype(jnp.bfloat16)
        serve_y(2)
        serve_x(3)
        complete(2)
        q[:p_rows, :] = (dot_plain(xp[...], weight(2)) + bias[0:1, :]).astype(jnp.bfloat16)
        q[p_rows:, :] = (dot_plain(xc[...], weight(2)) + bias[0:1, :]).astype(jnp.bfloat16)

        def keep(ref, target, i):
            return pltpu.make_async_copy(ref, target, out_sem.at[i])

        kept = [(q, q_out, 0), (kc, kc_out, 1), (vc, vc_out, 2)]
        for item in kept:
            keep(*item).start()

        def serve_kv(g):
            for t in range(2):
                remote(kv_part(t, g, there), kx_s.at[g, t], kx_r.at[g, t], across).wait_recv()
                kv_forward(t, g).start()

        def complete_kv(g):
            for t in range(2):
                remote(
                    kv_part(t, g, 2 * x + 1 - core), kc_s.at[g, t], kc_r.at[g, t], partner
                ).wait_recv()
                remote(kv_part(t, g, far), kd_s.at[g, t], kd_r.at[g, t], partner).wait_recv()

        serve_kv(0)
        arrive = {4: 26.3, 5: 27.9, 6: 35.2, 7: 36.8, 8: 44.1, 9: 45.7, 10: 48.9}
        work = [(33.6, serve_kv, 1), (42.4, serve_kv, 2), (27.0, serve_y, 3), (30.0, complete, 3)]
        for k in range(4, pieces):
            at = arrive[k]
            work.append((at, serve_x, k))
            if k in by_z:
                work += [(at + 4, serve_y, k), (at + 10, serve_z, k), (at + 13, complete, k)]
            else:
                work += [(at + 6, serve_y, k), (at + 9, complete, k)]
        slots = pairs * tiles
        work = [(max(0, round((at - 26) / 1.37 - 0.6)), act, k) for at, act, k in work]
        work.sort(key=lambda item: item[0])

        def att_store(p):
            lanes = pl.ds(pl.multiple_of(p * PAIR, PAIR), PAIR)
            return pltpu.make_async_copy(att.at[:, lanes], att_out.at[:, lanes], out_sem.at[5 + p])

        def pair(p, carry):
            @pl.when(p % 2 == 0)
            def _():
                complete_kv(p // 2)

            def between(tile):
                for slot, action, k in work:
                    if slot < slots and slot % tiles == tile:

                        @pl.when(p == slot // tiles)
                        def _(action=action, k=k):
                            action(k)

            lanes = pl.ds(pl.multiple_of(p * PAIR, PAIR), PAIR)
            attend_fwd_pair(
                shard,
                p_rows,
                q.at[:, lanes],
                kp.at[:, lanes],
                vp.at[:, lanes],
                kc.at[:, lanes],
                vc.at[:, lanes],
                att.at[:, lanes],
                lse.at[p],
                between,
            )
            att_store(p).start()
            return carry

        lax.fori_loop(0, pairs, pair, 0)
        kept += [(kp, kp_out, 3), (vp, vp_out, 4)]
        for item in kept[3:]:
            keep(*item).start()
        for slot, action, k in work:
            if slot >= slots:
                action(k)
        for item in kept:
            keep(*item).wait()

        def last_pair(p, carry):
            att_store(p).wait()
            return carry

        lax.fori_loop(0, pairs, last_pair, 0)
        for k in range(pieces):
            w_store(k).wait()
            for copy in (core_copy, x_copy, y_copy, d_copy, e_copy):
                copy(k).wait_send()
            if k in by_z:
                z_copy(k).wait_send()
        for g in range(chunks):
            for t in range(2):
                for copy in (kv_core, kv_across, kv_forward):
                    copy(t, g).wait_send()

    def sems(*dims):
        return pltpu.SemaphoreType.DMA(dims)

    def low(*dims):
        return jax.ShapeDtypeStruct(dims, jnp.bfloat16)

    anywhere = pl.BlockSpec(memory_space=pl.ANY)
    vmem = pl.BlockSpec(memory_space=pltpu.VMEM)
    n = pieces
    out = pl.pallas_call(
        kernel,
        in_specs=[vmem, vmem, anywhere, anywhere, anywhere, anywhere, vmem],
        out_specs=[anywhere] * 8 + [vmem],
        out_shape=[
            low(8, 4, rows, D),
            low(4, 3, rows, D),
            low(tokens, D),
            low(cont_len, D),
            low(cont_len, D),
            low(p_len, D),
            low(p_len, D),
            jax.ShapeDtypeStruct((tokens, D), jnp.float32),
            jax.ShapeDtypeStruct((pairs, 8, tokens), jnp.float32),
        ],
        scratch_shapes=[
            pltpu.VMEM((n, rows, D), jnp.float32),
            pltpu.VMEM((n, 4, rows, D), jnp.bfloat16),
            pltpu.VMEM((tokens, D), jnp.bfloat16),
            pltpu.VMEM((cont_len, D), jnp.bfloat16),
            pltpu.VMEM((cont_len, D), jnp.bfloat16),
            pltpu.VMEM((p_len, D), jnp.bfloat16),
            pltpu.VMEM((p_len, D), jnp.bfloat16),
            pltpu.VMEM((tokens, D), jnp.float32),
        ]
        + [sems(n)] * 14
        + [sems(chunks, 2)] * 6
        + [sems(5 + pairs)],
        compiler_params=pltpu.CompilerParams(
            collective_id=1, has_side_effects=True, vmem_limit_bytes=VMEM_ALL
        ),
        name="project_and_attend",
    )(prompt, conts, w_qkv, w_out, w_in, w_ffo, layer_biases)
    w_all, wf, q, kc, vc, kp, vp, att, lse = out
    w_all = w_all.reshape(8, 4 * rows, D)
    return w_all, wf.reshape(4, 3 * rows, D), q, kp, vp, kc, vc, att, lse


def project_native(prompt, conts, w_qkv, w_out, w_in, w_ffo, layer_biases):
    rows = prompt.shape[0]

    def gathered(value):
        return lax.all_gather(value.astype(jnp.bfloat16), "shard", axis=0, tiled=True)

    qkv, out, inner, ffo = (gathered(w) for w in (w_qkv, w_out, w_in, w_ffo))
    tokens = jnp.concatenate([prompt, conts], 0)
    bias = jnp.concatenate([layer_biases[0], jnp.zeros((D,), jnp.float32), layer_biases[1]])
    qkv_b = (dot_plain(tokens, qkv) + bias).astype(jnp.bfloat16)
    q, keys, values = (qkv_b[:, i * D : (i + 1) * D] for i in range(3))
    kp, vp = gathered(keys[:rows]), gathered(values[:rows])
    kc, vc = keys[rows:], values[rows:]
    att, lse = attend_forward(q, kp, vp, kc, vc, rows)
    blocks = [qkv[:, D : 2 * D], qkv[:, 2 * D :], qkv[:, :D], out]
    blocks += [inner[:, i * D : (i + 1) * D] for i in range(inner.shape[1] // D)]
    return jnp.stack(blocks), ffo, q, kp, vp, kc, vc, att, lse


def student_head(label, stu, vectors, w_pool, w_class, bias_class, classes):
    part_w = STU // SHEADS
    low_half = lax.broadcasted_iota(jnp.int32, stu.shape, 1) < part_w
    row_low = lax.broadcasted_iota(jnp.int32, (1, STU), 1) < part_w
    query, bias_pool = vectors[1:2, :], vectors[2:3, :]

    def by_head(values):
        low_sum = jnp.sum(jnp.where(low_half[: values.shape[0]], values, 0.0), 1, keepdims=True)
        high_sum = jnp.sum(jnp.where(low_half[: values.shape[0]], 0.0, values), 1, keepdims=True)
        return jnp.where(low_half[: values.shape[0]], low_sum, high_sum)

    scores = by_head(stu * query) * part_w ** (-0.5)
    largest = jnp.max(scores, 0, keepdims=True)
    expo = jnp.exp(scores - largest)
    weights = expo / jnp.sum(expo, 0, keepdims=True)
    pooled = jnp.sum(weights * stu, 0, keepdims=True)

    square = (STU, STU)
    on_diagonal = lax.broadcasted_iota(jnp.int32, square, 0) == lax.broadcasted_iota(
        jnp.int32, square, 1
    )

    def column(row):
        return jnp.sum(jnp.where(on_diagonal, row, 0.0), 1, keepdims=True)

    def times(row, matrix):
        return jnp.sum(column(row) * matrix, 0, keepdims=True)

    def times_turned(row, matrix):
        total = jnp.sum(matrix * row, 1, keepdims=True)
        return jnp.sum(jnp.where(on_diagonal, total, 0.0), 0, keepdims=True)

    top = jnp.tanh(times(pooled, w_pool) + bias_pool)
    lane = lax.broadcasted_iota(jnp.int32, (1, STU), 1)
    logits = times(top, w_class) + bias_class
    seen = jnp.where(lane < classes, logits, NEG_BIG)
    expo_l = jnp.exp(seen - jnp.max(seen, 1, keepdims=True))
    g_logits = expo_l / jnp.sum(expo_l, 1, keepdims=True) - jnp.where(lane == label, 1.0, 0.0)
    g_class = column(top) * g_logits
    g_pre = times_turned(g_logits, w_class) * (1.0 - top * top)
    g_pool = column(pooled) * g_pre
    g_pooled = times_turned(g_pre, w_pool)
    g_weights = by_head(stu * g_pooled)
    mean = jnp.sum(weights * g_weights, 0, keepdims=True)
    g_scores = weights * (g_weights - mean) * part_w ** (-0.5)
    g_stu = weights * g_pooled + g_scores * query
    g_query = jnp.sum(g_scores * stu, 0, keepdims=True)
    return logits, g_stu, g_query, g_pre, g_pool, g_class, g_logits


def middle(
    ahead, att, prompt, conts, prompt_cot, cont_cot, labels, w_all, wf, wf_rows,
    biases, gains, bias_in, student, vectors, w_pool, w_class, bias_class,
):
    p_rows, cont_len = prompt.shape[0], conts.shape[0]
    tokens = p_rows + cont_len
    ff = bias_in.shape[0]
    blocks = ff // D
    steps = tokens // TILE
    wide = D // TILE
    classes = w_class.shape[1]
    w_class_p = jnp.pad(w_class, ((0, 0), (0, STU - classes)))
    bias_class_p = jnp.pad(bias_class[None], ((0, 0), (0, STU - classes)))
    g_names = 2 * blocks + 1

    def kernel(
        label_ref, att_h, xp, xc, cp, cc, w_h, wf_h, wf_own, bias, gain, b_in, w_stu, vec, w_p, w_c, b_c,
        out_p, out_c, logits_out, grads_h, g_r1_h, g_att_h, small, totals_h,
        x_v, cot_v, out_v, att_v, att_b, w_v, wf_v, norm1, norm2, rstd1, rstd2, x1_b, act, slope, g_res, g_ffn, g_br, g_stu_b, grads,
        sums, in_sum, load, store, *links,
    ):
        def fetch(source, target, i):
            return pltpu.make_async_copy(source, target, load.at[i])

        loads = [
            fetch(att_h, att_v, 0),
            fetch(w_h.at[3], w_v.at[0], 1),
            fetch(w_h.at[pl.ds(4, blocks)], w_v.at[pl.ds(1, blocks)], 2),
            fetch(wf_h, wf_v.at[:, : wf_h.shape[1]], 3),
            fetch(xp, x_v.at[:p_rows], 4),
            fetch(xc, x_v.at[p_rows:], 5),
            fetch(cp, cot_v.at[:p_rows], 6),
            fetch(cc, cot_v.at[p_rows:], 7),
        ]
        for copy in loads:
            copy.start()
        rows = D // blocks
        if ahead:
            (stage, cr, xr, w_s, w_r, c_s, c_r, x_s, x_r) = links
            own_rows = fetch(wf_own.at[pl.ds(D - rows, rows), :], stage, 8)
            own_rows.start()
            rep, shard = lax.axis_index("rep"), lax.axis_index("shard")
            z, y = rep // 2, rep % 2
            x, core = shard // 2, shard % 2
            partner = (rep, 2 * x + 1 - core)
            across = (rep, 2 * (1 - x) + core)
            beside = (2 * z + 1 - y, shard)
            there, far = 2 * (1 - x) + core, 2 * (1 - x) + 1 - core
            barrier = pltpu.get_barrier_semaphore()
            for other in (partner, across, beside):
                pl.semaphore_signal(barrier, inc=1, device_id=other, device_id_type=MESH_ID)
            pl.semaphore_wait(barrier, 3)

            def remote(source, target, send, recv, device):
                return pltpu.make_async_remote_copy(
                    src_ref=source,
                    dst_ref=target,
                    send_sem=send,
                    recv_sem=recv,
                    device_id=device,
                    device_id_type=MESH_ID,
                )

            def moved(i, block, which, device):
                first = D - rows
                at = pl.ds(first, rows)
                if which is not None:
                    half = rows // 2
                    at = pl.ds(pl.multiple_of(first + which * half, 16), half)
                ref = wf_v.at[block, at, :]
                return remote(ref, ref, w_s.at[i], w_r.at[i], device)

            def core_copy(k, xx):
                block = pl.ds(pl.multiple_of((2 * xx + 1 - core) * rows, 16), rows)
                return remote(
                    grads.at[k, block, :], cr.at[k, xx], c_s.at[k, xx], c_r.at[k, xx], partner
                )

            def mine(xx):
                return pl.ds(pl.multiple_of((2 * xx + core) * rows, 16), rows)

            def x_copy(k):
                return remote(grads.at[k, mine(1 - x), :], xr.at[k], x_s.at[k], x_r.at[k], across)

            own_rows.wait()
            wf_v[shard, D - rows :, :] = stage[...].astype(jnp.bfloat16)
            moved(1, shard, y, across).start()
            moved(0, shard, None, partner).start()

        def serve_across():
            moved(1, there, y, across).wait_recv()
            moved(2, there, y, beside).start()
            moved(3, there, y, partner).start()

        def serve_beside():
            moved(2, there, 1 - y, beside).wait_recv()
            moved(4, there, 1 - y, partner).start()

        def gathered():
            moved(0, 2 * x + 1 - core, None, partner).wait_recv()
            moved(3, far, y, partner).wait_recv()
            moved(4, far, 1 - y, partner).wait_recv()

        def stage_x():
            for k in range(ahead):
                for xx in range(2):
                    core_copy(k, xx).wait_recv()
                block = mine(1 - x)
                total = grads[k, block, :].astype(jnp.float32) + cr[k, 1 - x].astype(jnp.float32)
                grads[k, block, :] = total.astype(jnp.bfloat16)
                x_copy(k).start()

        sums[...] = jnp.zeros_like(sums)
        small[...] = jnp.zeros_like(small)

        def row(i):
            return pl.ds(pl.multiple_of(i * TILE, TILE), TILE)

        def loop(count):
            def run(step):
                def body(i, carry):
                    step(i)
                    return carry

                lax.fori_loop(0, count, body, 0)

            return run

        def normalize(values):
            center = values - jnp.mean(values, -1, keepdims=True)
            spread = jnp.mean(center * center, -1, keepdims=True)
            scale = lax.rsqrt(spread + 1e-05)
            return center * scale, scale

        def norm_back(g, gain_row, hat, scale):
            gg = g * gain_row
            return scale * (
                gg
                - jnp.mean(gg, -1, keepdims=True)
                - hat * jnp.mean(gg * hat, -1, keepdims=True)
            )

        def add_sum(i, values):
            sums[i : i + 1, :] += jnp.sum(values, 0, keepdims=True)

        for i in (0, 1, 4, 5):
            loads[i].wait()

        @loop(steps)
        def _(i):
            part = att_v[row(i), :].astype(jnp.bfloat16)
            att_b[row(i), :] = part
            branch = dot_plain(part, w_v[0]) + bias[2:3, :]
            hat, scale = normalize(x_v[row(i), :].astype(jnp.float32) + branch)
            norm1[row(i), :] = hat
            rstd1[row(i), :] = jnp.broadcast_to(scale, (TILE, 128))
            x1_b[row(i), :] = (hat * gain[0:1, :] + bias[4:5, :]).astype(jnp.bfloat16)

        loads[2].wait()

        def inner(i, carry):
            lanes = pl.ds(pl.multiple_of(lax.rem(i, wide) * TILE, TILE), TILE)
            columns = pl.ds(pl.multiple_of(i * TILE, TILE), TILE)
            hidden = dot_plain(x1_b[...], w_v[1 + i // wide, :, lanes]) + b_in[:, columns]
            cdf = 0.5 * (1.0 + lax.erf(hidden * 2.0 ** (-0.5)))
            act[:, columns] = (hidden * cdf).astype(jnp.bfloat16)
            density = jnp.exp(hidden * hidden * (-0.5)) * 0.3989422804014327
            slope[:, columns] = (cdf + hidden * density).astype(jnp.bfloat16)
            if ahead:
                pl.when(i == 3)(serve_across)
                pl.when(i == 10)(serve_beside)
            return carry

        lax.fori_loop(0, ff // TILE, inner, 0)
        loads[3].wait()
        if ahead:
            gathered()

        @loop(steps)
        def _(i):
            ffn = bias[3:4, :]
            for j in range(blocks):
                ffn = ffn + dot_plain(act[row(i), j * D : (j + 1) * D], wf_v[j])
            first = norm1[row(i), :] * gain[0:1, :] + bias[4:5, :]
            hat, scale = normalize(first + ffn)
            norm2[row(i), :] = hat
            rstd2[row(i), :] = jnp.broadcast_to(scale, (TILE, 128))
            out_v[row(i), :] = (hat * gain[1:2, :] + bias[5:6, :]).astype(jnp.bfloat16)

        out_stores = [
            pltpu.make_async_copy(out_v.at[:p_rows], out_p, store.at[g_names + 2]),
            pltpu.make_async_copy(out_v.at[p_rows:], out_c, store.at[g_names + 3]),
        ]
        for copy in out_stores:
            copy.start()
        base = 8 * (D // 128) + ff // 128
        w_stu_b = w_stu[...].astype(jnp.bfloat16)

        @pl.when(lax.axis_index("rep") >= 0)
        def _():
            stu = dot_plain(out_v[p_rows:, :], w_stu_b) + vec[0:1, :]
            logits, g_stu, g_query, g_pre, g_pool, g_class, g_logits = student_head(
                label_ref[0, 0], stu, vec, w_p[...], w_c[...], b_c[...], classes
            )
            logits_out[...] = logits[:, :classes]
            low = g_stu.astype(jnp.bfloat16)
            g_stu_b[:p_rows, :] = jnp.zeros((p_rows, STU), jnp.bfloat16)
            g_stu_b[p_rows:, :] = low
            small[base : base + 1, STU:] = jnp.sum(low.astype(jnp.float32), 0, keepdims=True)
            small[base + 1 : base + 2, STU:] = g_query
            small[base + 2 : base + 3, STU:] = g_pre
            small[base + 3 : base + 4, STU:] = g_logits
            small[base + 8 : base + 8 + STU, STU:] = g_pool
            small[base + 8 + STU : base + 8 + 2 * STU, STU:] = g_class

        small[:, :STU] = dot_first(out_v[p_rows:, :], g_stu_b[p_rows:, :])
        loads[6].wait()
        loads[7].wait()

        @loop(steps)
        def _(i):
            g = cot_v[row(i), :].astype(jnp.float32) + dot_second(g_stu_b[row(i), :], w_stu_b)
            hat = norm2[row(i), :]
            add_sum(7, g * hat)
            add_sum(5, g)
            g_r2 = norm_back(g, gain[1:2, :], hat, rstd2[row(i), :1])
            g_res[row(i), :] = g_r2
            low = g_r2.astype(jnp.bfloat16)
            g_ffn[row(i), :] = low
            add_sum(3, low.astype(jnp.float32))

        def piece_store(k):
            return pltpu.make_async_copy(grads.at[k], grads_h.at[k], store.at[k])


        @loop(blocks)
        def _(j):
            columns = pl.ds(pl.multiple_of(j * D, D), D)
            product = dot_first(act[:, columns], g_ffn[...]).astype(jnp.bfloat16)
            for k in range(blocks):
                target = pl.ds(pl.multiple_of(j * rows, 16), rows)
                grads[k, target, :] = product[k * rows : (k + 1) * rows]

        for k in range(ahead):
            for xx in range(2):
                core_copy(k, xx).start()
        for k in range(ahead, blocks):
            piece_store(k).start()


        in_sum[...] = jnp.zeros_like(in_sum)

        @loop(steps)
        def _(i):
            for j in range(blocks):
                columns = slice(j * D, (j + 1) * D)
                g_act = dot_second(g_ffn[row(i), :], wf_v[j])
                low = (g_act * slope[row(i), columns].astype(jnp.float32)).astype(jnp.bfloat16)
                slope[row(i), columns] = low
                in_sum[:, columns] += jnp.sum(low.astype(jnp.float32), 0, keepdims=True)
            if ahead:
                pl.when(i == 0)(stage_x)

        @loop(blocks)
        def _(j):
            columns = pl.ds(pl.multiple_of(j * D, D), D)
            grads[blocks + j] = dot_first(x1_b[...], slope[:, columns]).astype(jnp.bfloat16)
            piece_store(blocks + j).start()

        @loop(steps)
        def _(i):
            g = g_res[row(i), :]
            for j in range(blocks):
                g += dot_second(slope[row(i), j * D : (j + 1) * D], w_v[1 + j])
            hat = norm1[row(i), :]
            add_sum(6, g * hat)
            add_sum(4, g)
            g_r1 = norm_back(g, gain[0:1, :], hat, rstd1[row(i), :1])
            g_res[row(i), :] = g_r1
            low = g_r1.astype(jnp.bfloat16)
            g_br[row(i), :] = low
            add_sum(2, low.astype(jnp.float32))

        res_store = pltpu.make_async_copy(g_res, g_r1_h, store.at[g_names])
        res_store.start()
        g_ffn[...] = dot_second(g_br[...], w_v[0]).astype(jnp.bfloat16)
        att_store = pltpu.make_async_copy(g_ffn, g_att_h, store.at[g_names + 1])
        att_store.start()
        grads[2 * blocks] = dot_first(att_b[...], g_br[...]).astype(jnp.bfloat16)
        piece_store(2 * blocks).start()
        spread = D // 128
        for i in range(8):
            for part in range(spread):
                small[i * spread + part : i * spread + part + 1, STU:] = sums[
                    i : i + 1, part * 128 : (part + 1) * 128
                ]
        for part in range(ff // 128):
            at = 8 * spread + part
            small[at : at + 1, STU:] = in_sum[:, part * 128 : (part + 1) * 128]
        res_store.wait()
        att_store.wait()
        for copy in out_stores:
            copy.wait()
        for k in range(ahead):
            x_copy(k).wait_recv()
            total = grads[k, mine(x), :].astype(jnp.float32) + cr[k, x].astype(jnp.float32)
            cr[k, x] = (total + xr[k].astype(jnp.float32)).astype(jnp.bfloat16)
            pltpu.make_async_copy(cr.at[k, x], totals_h.at[k], store.at[k]).start()
        for k in range(ahead, g_names):
            piece_store(k).wait()
        for k in range(ahead):
            pltpu.make_async_copy(cr.at[k, x], totals_h.at[k], store.at[k]).wait()
            for xx in range(2):
                core_copy(k, xx).wait_send()
            x_copy(k).wait_send()
        if ahead:
            moved(0, shard, None, partner).wait_send()
            moved(1, shard, y, across).wait_send()
            moved(2, there, y, beside).wait_send()
            moved(3, there, y, partner).wait_send()
            moved(4, there, 1 - y, partner).wait_send()

    anywhere = pl.BlockSpec(memory_space=pl.ANY)
    vmem = pl.BlockSpec(memory_space=pltpu.VMEM)
    low = jnp.bfloat16

    def shaped(dims, kind=jnp.float32):
        return jax.ShapeDtypeStruct(dims, kind)

    params = pltpu.CompilerParams(vmem_limit_bytes=VMEM_ALL)
    link_scratch = []
    if ahead:
        params = pltpu.CompilerParams(
            collective_id=3, has_side_effects=True, vmem_limit_bytes=VMEM_ALL
        )
        piece = (D // blocks, D)
        link_scratch = [
            pltpu.VMEM(piece, jnp.float32),
            pltpu.VMEM((ahead, 2, *piece), low),
            pltpu.VMEM((ahead, *piece), low),
        ]
        link_scratch += [pltpu.SemaphoreType.DMA((5,))] * 2
        link_scratch += [pltpu.SemaphoreType.DMA((ahead, 2))] * 2
        link_scratch += [pltpu.SemaphoreType.DMA((ahead,))] * 2

    return pl.pallas_call(
        kernel,
        in_specs=[pl.BlockSpec(memory_space=pltpu.SMEM), anywhere]
        + [anywhere] * 7
        + [vmem] * 8,
        out_specs=[anywhere, anywhere, vmem, anywhere, anywhere, anywhere, vmem, anywhere],
        out_shape=[
            shaped((p_rows, D), low),
            shaped((cont_len, D), low),
            shaped((1, classes)),
            shaped((g_names, D, D), low),
            shaped((tokens, D)),
            shaped((tokens, D), low),
            shaped((D, 2 * STU)),
            shaped((max(ahead, 1), D // blocks, D), low),
        ],
        scratch_shapes=[
            pltpu.VMEM((tokens, D), low),
            pltpu.VMEM((tokens, D), low),
            pltpu.VMEM((tokens, D), low),
            pltpu.VMEM((tokens, D), jnp.float32),
            pltpu.VMEM((tokens, D), low),
            pltpu.VMEM((1 + blocks, D, D), low),
            pltpu.VMEM((blocks, D, D), low),
            pltpu.VMEM((tokens, D), jnp.float32),
            pltpu.VMEM((tokens, D), jnp.float32),
            pltpu.VMEM((tokens, 128), jnp.float32),
            pltpu.VMEM((tokens, 128), jnp.float32),
            pltpu.VMEM((tokens, D), low),
            pltpu.VMEM((tokens, ff), low),
            pltpu.VMEM((tokens, ff), low),
            pltpu.VMEM((tokens, D), jnp.float32),
            pltpu.VMEM((tokens, D), low),
            pltpu.VMEM((tokens, D), low),
            pltpu.VMEM((tokens, STU), low),
            pltpu.VMEM((g_names, D, D), low),
            pltpu.VMEM((8, D), jnp.float32),
            pltpu.VMEM((1, ff), jnp.float32),
            pltpu.SemaphoreType.DMA((9,)),
            pltpu.SemaphoreType.DMA((g_names + 4,)),
        ]
        + link_scratch,
        compiler_params=params,
        name="middle",
    )(
        labels,
        att,
        prompt,
        conts,
        prompt_cot,
        cont_cot,
        w_all,
        wf,
        wf_rows,
        biases,
        gains,
        bias_in[None],
        student,
        vectors,
        w_pool,
        w_class_p,
        bias_class_p,
    )


def sum_native(g9, g_qkvw, small):
    blocks = (g9.shape[0] - 1) // 2
    rows = D // blocks
    ffo = g9[:blocks].reshape(blocks, blocks, rows, D).transpose(1, 0, 2, 3).reshape(-1, D)
    inner = jnp.concatenate([g9[blocks + j] for j in range(blocks)], 1)

    def over(grad):
        part = lax.psum_scatter(
            grad.astype(jnp.bfloat16), "shard", scatter_dimension=0, tiled=True
        )
        return lax.psum(part, "rep").astype(jnp.float32)

    owned = tuple(over(grad) for grad in (g_qkvw, g9[2 * blocks], inner, ffo))
    return owned, lax.psum(small, ("rep", "shard"))


def finish(
    ahead, totals, q, kp, vp, kc, vc, att, lse, g_att, g9, g_resid, small, w_all, prompt, conts, ff
):
    pieces, ready = 12, 9
    p_rows, cont_len = prompt.shape[0], conts.shape[0]
    tokens = p_rows + cont_len
    p_len = kp.shape[0]
    pairs = HEADS // 2
    rows = D // 4
    half, quarter = D // 2, rows // 4
    s_width = small.shape[1]
    chunk = 2 * PAIR
    chunks = D // chunk
    across_lanes = D // 128

    def kernel(
        q_h, kp_h, vp_h, kc_h, vc_h, att_h, g_att_h, g9, g_res_h, w_h, totals_h, ls, sm, xp, xc,
        out_pg, out_cg, out_q, out_o, out_i, out_f, fin_s,
        qv, kpv, vpv, kcv, vcv, attv, gav, accum, dq, dkp, dvp, dkc, dvc, kr, kx, kvs, wv, g_tok, made, head,
        own, cr, xr, yr, zr, fb, made_s, own_s, cr_s, xr_s, yr_s, zr_s, fb_s,
        load, sem_own, c_send, c_recv, x_send, x_recv, y_send, y_recv, z_send, z_recv,
        f_send, f_recv, o_send, o_recv, o_own, g_send, g_recv, kc_s, kc_r, kx_s, kx_r, out_sem,
    ):
        rep, shard = lax.axis_index("rep"), lax.axis_index("shard")
        z, y = rep // 2, rep % 2
        x, core = shard // 2, shard % 2
        partner = (rep, 2 * x + 1 - core)
        across = (rep, 2 * (1 - x) + core)
        beside = (2 * z + 1 - y, shard)
        far = (rep, 2 * (1 - x) + 1 - core)

        def along(step):
            return (2 * lax.rem(z + step, 4) + y, shard)

        def own_copy(k, xx):
            return pltpu.make_async_copy(
                g9.at[k, pl.ds(pl.multiple_of((2 * xx + core) * rows, 16), rows), :],
                own.at[k, xx],
                sem_own.at[k, xx],
            )

        fetched = [(q_h, qv), (kp_h, kpv), (vp_h, vpv), (kc_h, kcv), (vc_h, vcv)]
        fetched += [(att_h, attv), (g_att_h, gav), (w_h.at[pl.ds(0, 3)], wv), (g_res_h, g_tok)]

        def fetch(i):
            return pltpu.make_async_copy(*fetched[i], load.at[i])

        def total_copy(k):
            return pltpu.make_async_copy(totals_h.at[k], own.at[k, x], sem_own.at[k, 0])

        for k in range(ahead):
            total_copy(k).start()
        for k in range(ahead, ahead + 2):
            for xx in range(2):
                own_copy(k, xx).start()
        for i in range(7):
            fetch(i).start()
        for k in range(ahead + 2, ready):
            for xx in range(2):
                own_copy(k, xx).start()
        for i in (7, 8):
            fetch(i).start()

        barrier = pltpu.get_barrier_semaphore()
        others = [partner, across, beside, along(1), along(2), along(3), far]
        for other in others:
            pl.semaphore_signal(barrier, inc=1, device_id=other, device_id_type=MESH_ID)
        pl.semaphore_wait(barrier, len(others))

        def remote(source, target, send, recv, device):
            return pltpu.make_async_remote_copy(
                src_ref=source,
                dst_ref=target,
                send_sem=send,
                recv_sem=recv,
                device_id=device,
                device_id_type=MESH_ID,
            )

        big = (own, cr, xr, yr, zr, fb, half)
        narrow = (own_s, cr_s, xr_s, yr_s, zr_s, fb_s, s_width // 2)

        def bufs(k):
            if isinstance(k, int) and k == pieces:
                return narrow, 0
            return big, k

        def core_copy(k, xx):
            b, i = bufs(k)
            block = 2 * xx + 1 - core
            if not isinstance(k, int):
                source = b[1].at[i, xx]
            elif k < ready:
                source = g9.at[k, pl.ds(pl.multiple_of(block * rows, 16), rows), :]
            elif k < pieces:
                source = made.at[k - ready, block]
            else:
                source = made_s.at[block]
            return remote(source, b[1].at[i, xx], c_send.at[k, xx], c_recv.at[k, xx], partner)

        def x_copy(k):
            b, i = bufs(k)
            return remote(b[0].at[i, 1 - x], b[2].at[i], x_send.at[k], x_recv.at[k], across)

        def lanes_of(b, which):
            return pl.ds(pl.multiple_of(which * b[6], 128), b[6])

        def y_copy(k):
            b, i = bufs(k)
            source = b[0].at[i, x, :, lanes_of(b, 1 - y)]
            return remote(source, b[3].at[i], y_send.at[k], y_recv.at[k], beside)

        def rows_of(which):
            return pl.ds(pl.multiple_of(which * quarter, 16), quarter)

        def zs_copy(k, step):
            b, i = bufs(k)
            source = b[0].at[i, x, rows_of(lax.rem(z + step, 4)), lanes_of(b, y)]
            return remote(
                source, b[4].at[i, z], z_send.at[k, step - 1], z_recv.at[k, z], along(step)
            )

        def zr_wait(k, step):
            b, i = bufs(k)
            slot = lax.rem(z + step, 4)
            target = b[4].at[i, slot]
            remote(
                target, target, z_send.at[k, step - 1], z_recv.at[k, slot], along(step)
            ).wait_recv()

        def fs_copy(k, step):
            b, i = bufs(k)
            block = b[5].at[i, rows_of(z), :]
            return remote(block, block, f_send.at[k, step - 1], f_recv.at[k, z], along(step))

        def fr_wait(k, step):
            b, i = bufs(k)
            slot = lax.rem(z + step, 4)
            block = b[5].at[i, rows_of(slot), :]
            remote(
                block, block, f_send.at[k, step - 1], f_recv.at[k, slot], along(step)
            ).wait_recv()

        def final(k, yy):
            b, _ = bufs(k)
            if k < 4:
                return out_f.at[k * rows : (k + 1) * rows, lanes_of(b, yy)]
            if k == 8:
                return out_o.at[:, lanes_of(b, yy)]
            if k == pieces:
                return fin_s.at[shard, :, lanes_of(b, yy)]
            out, at = (out_i, (k - 4) * D) if k < 8 else (out_q, (k - 9) * D)
            return out.at[:, pl.ds(pl.multiple_of(at + yy * half, 128), half)]

        def o_copy(k):
            b, i = bufs(k)
            return remote(b[5].at[i], final(k, y), o_send.at[k], o_recv.at[k], beside)

        def o_wait(k):
            b, i = bufs(k)
            remote(b[5].at[i], final(k, 1 - y), o_send.at[k], o_recv.at[k], beside).wait_recv()

        def o_local(k):
            b, i = bufs(k)
            return pltpu.make_async_copy(b[5].at[i], final(k, y), o_own.at[k])

        def wide(value):
            return value.astype(jnp.float32)

        def stage_x(k):
            b, i = bufs(k)
            for xx in range(2):
                core_copy(k, xx).wait_recv()
                if not isinstance(k, int):
                    pl.when(k < ready)(own_copy(k, xx).wait)
            b[0][i, 1 - x] = (wide(b[0][i, 1 - x]) + wide(b[1][i, 1 - x])).astype(jnp.bfloat16)
            x_copy(k).start()

        def stage_y(k):
            b, i = bufs(k)
            x_copy(k).wait_recv()
            total = wide(b[0][i, x]) + wide(b[1][i, x]) + wide(b[2][i])
            b[0][i, x] = total.astype(jnp.bfloat16)
            y_copy(k).start()

        def stage_z(k):
            b, i = bufs(k)
            y_copy(k).wait_recv()
            lanes = lanes_of(b, y)
            total = wide(b[0][i, x, :, lanes]) + wide(b[3][i])
            b[0][i, x, :, lanes] = total.astype(jnp.bfloat16)
            for step in (2, 1, 3):
                zs_copy(k, step).start()

        def stage_f(k):
            b, i = bufs(k)
            total = wide(b[0][i, x, rows_of(z), lanes_of(b, y)])
            for step in (1, 2, 3):
                zr_wait(k, step)
                total += wide(b[4][i, lax.rem(z + step, 4)])
            b[5][i, rows_of(z), :] = total.astype(jnp.bfloat16)
            for step in (2, 1, 3):
                fs_copy(k, step).start()

        def stage_o(k):
            for step in (1, 2, 3):
                fr_wait(k, step)
            for kk in range(pieces + 1) if not isinstance(k, int) else [k]:

                def begin(kk=kk):
                    o_copy(kk).start()
                    o_local(kk).start()

                if isinstance(k, int):
                    begin()
                else:
                    pl.when(k == kk)(begin)

        def send_core(k):
            for xx in range(2):
                core_copy(k, xx).start()

        for k in range(ahead, ready):
            send_core(k)

        def stages_x(first, last):
            def step(k, carry):
                stage_x(k)
                return carry

            lax.fori_loop(first, last, step, 0)

        for k in range(ahead):
            total_copy(k).wait()
            y_copy(k).start()
        stages_x(ahead, ahead + 2)
        kv = (dkp, dvp)

        def kv_rows(block):
            return pl.ds(pl.multiple_of(block * p_rows, p_rows), p_rows)

        def kv_lanes(g):
            return pl.ds(g * chunk if isinstance(g, int) else pl.multiple_of(g * chunk, chunk), chunk)

        def kv_core(t, g, xx):
            return remote(
                kv[t].at[kv_rows(2 * xx + 1 - core), kv_lanes(g)],
                kr.at[t, xx, :, kv_lanes(g)],
                kc_s.at[g, t, xx],
                kc_r.at[g, t, xx],
                partner,
            )

        def kv_across(t, g):
            return remote(
                kv[t].at[kv_rows(2 * (1 - x) + core), kv_lanes(g)],
                kx.at[t, :, kv_lanes(g)],
                kx_s.at[g, t],
                kx_r.at[g, t],
                across,
            )

        def serve_kv(g):
            block, lanes = kv_rows(2 * (1 - x) + core), kv_lanes(g)
            for t in range(2):
                for xx in range(2):
                    kv_core(t, g, xx).wait_recv()
                total = wide(kv[t][block, lanes]) + wide(kr[t, 1 - x, :, lanes])
                kv[t][block, lanes] = total.astype(jnp.bfloat16)
                kv_across(t, g).start()

        for i in range(7):
            fetch(i).wait()

        def pair(p, carry):
            def between(index):
                if index == 0:
                    pl.when(p + ahead + 2 < ready)(lambda: stage_x(p + ahead + 2))
                if index == 1:
                    pl.when((p == 2) | (p == 4))(lambda: serve_kv(p // 2 - 1))
                if index == 2:
                    pl.when(p >= 1)(lambda: stage_y(p + ahead - 1))
                if index == 3:
                    stage_z(p)
                if index == 4:
                    pl.when(p >= 1)(lambda: stage_f(p - 1))
                if index == 5:
                    pl.when(p >= 2)(lambda: stage_o(p - 2))

            lanes = pl.ds(pl.multiple_of(p * PAIR, PAIR), PAIR)

            def cut(ref):
                return ref.at[:, lanes]

            attend_bwd_pair(
                shard, p_rows, cut(qv), cut(kpv), cut(vpv), cut(kcv), cut(vcv), cut(gav), cut(attv),
                ls.at[p], cut(dq), cut(dkp), cut(dvp), cut(dkc), cut(dvc), accum, between,
            )

            @pl.when(p % 2 == 1)
            def _():
                for t in range(2):
                    for xx in range(2):
                        kv_core(t, p // 2, xx).start()

            return carry

        lax.fori_loop(0, pairs, pair, 0)

        def keep_piece(k, product):
            for block in range(4):
                made[k - ready, block] = product[block * rows : (block + 1) * rows]
            for xx in range(2):
                own[k, xx] = made[k - ready, 2 * xx + core]
            send_core(k)

        product = dot_first(xp[...], dq[:p_rows, :]) + dot_first(xc[...], dq[p_rows:, :])
        keep_piece(9, product.astype(jnp.bfloat16))
        serve_kv(chunks - 1)
        for i in (7, 8):
            fetch(i).wait()
        stages_x(9, 10)
        g_tok[...] += dot_second(dq[...], wv[2])
        stores = [
            pltpu.make_async_copy(g_tok.at[:p_rows, :], out_pg, out_sem.at[0]),
            pltpu.make_async_copy(g_tok.at[p_rows:, :], out_cg, out_sem.at[1]),
        ]

        def with_kv():
            for g in range(chunks):
                for t in range(2):
                    kv_across(t, g).wait_recv()
            for t in range(2):
                total = wide(kv[t][kv_rows(shard), :]) + wide(kr[t, x]) + wide(kx[t])
                kvs[t] = total.astype(jnp.bfloat16)
            g_bias = jnp.sum(wide(dq[...]), 0, keepdims=True)
            v_bias = jnp.sum(wide(dvc[...]), 0, keepdims=True)
            v_bias += jnp.sum(wide(kvs[1]), 0, keepdims=True)
            head[...] = sm[:16, :]
            for part in range(across_lanes):
                lanes = slice(part * 128, (part + 1) * 128)
                head[part : part + 1, STU:] = g_bias[:, lanes]
                head[across_lanes + part : across_lanes + part + 1, STU:] = v_bias[:, lanes]
            for block in range(4):
                made_s[block] = sm[block * rows : (block + 1) * rows, :].astype(jnp.bfloat16)
            made_s[0, :16] = head[...].astype(jnp.bfloat16)
            for xx in range(2):
                own_s[0, xx] = made_s[2 * xx + core]
            send_core(pieces)
            for t in range(2):
                product = dot_first(xp[...], kvs[t]) + dot_first(xc[...], (dkc, dvc)[t][...])
                keep_piece(10 + t, product.astype(jnp.bfloat16))
            stage_x(pieces)
            stages_x(10, 12)
            g_tok[:p_rows, :] += dot_second(kvs[0], wv[0]) + dot_second(kvs[1], wv[1])
            for copy in stores:
                copy.start()

        def cont_part():
            g_tok[p_rows:, :] += dot_second(dkc[...], wv[0]) + dot_second(dvc[...], wv[1])

        def tick(n, carry):
            pl.when(n == 9)(with_kv)
            pl.when((n >= 8) & (n < pieces))(lambda: stage_y(n))
            pl.when(n == 10)(lambda: stage_y(pieces))
            pl.when(n < pieces + 1)(lambda: stage_z(n - 1))
            pl.when(n == 11)(lambda: stage_z(pieces))
            pl.when(n < pieces + 2)(lambda: stage_f(n - 2))
            pl.when(n == 12)(lambda: stage_f(pieces))
            stage_o(n - 3)
            pl.when(n == 13)(lambda: stage_o(pieces))
            pl.when(n == 7)(cont_part)
            return carry

        def g_copy(step):
            return remote(
                fin_s.at[shard],
                fin_s.at[shard],
                g_send.at[step - 1],
                g_recv.at[shard],
                (rep, lax.rem(shard + step, 4)),
            )

        def stage_g():
            o_wait(pieces)
            o_local(pieces).wait()
            for step in (1, 2, 3):
                g_copy(step).start()

        lax.fori_loop(pieces - 5, pieces + 3, tick, 0)
        stage_g()
        for step in (1, 2, 3):
            slot = lax.rem(shard + step, 4)
            remote(
                fin_s.at[slot], fin_s.at[slot], g_send.at[step - 1], g_recv.at[slot], far
            ).wait_recv()

        for k in range(pieces):
            o_wait(k)
            o_local(k).wait()
        for copy in stores:
            copy.wait()

        def sent(k):
            def two():
                for xx in range(2):
                    core_copy(k, xx).wait_send()
                x_copy(k).wait_send()

            if isinstance(k, int):
                two()
            else:
                pl.when(k >= ahead)(two)
            y_copy(k).wait_send()
            for step in (1, 2, 3):
                zs_copy(k, step).wait_send()
                fs_copy(k, step).wait_send()

        def sent_step(k, carry):
            sent(k)
            return carry

        lax.fori_loop(0, pieces, sent_step, 0)
        sent(pieces)
        for k in range(pieces + 1):
            o_copy(k).wait_send()
        for step in (1, 2, 3):
            g_copy(step).wait_send()
        for g in range(chunks):
            for t in range(2):
                for xx in range(2):
                    kv_core(t, g, xx).wait_send()
                kv_across(t, g).wait_send()

    def sems(*dims):
        return pltpu.SemaphoreType.DMA(dims)

    def low(*dims):
        return pltpu.VMEM(dims, jnp.bfloat16)

    def full(*dims):
        return pltpu.VMEM(dims, jnp.float32)

    def buffers(count, columns):
        cut = columns // 2
        return [
            low(count, 2, rows, columns),
            low(count, 2, rows, columns),
            low(count, rows, columns),
            low(count, rows, cut),
            low(count, 4, quarter, cut),
            low(count, rows, cut),
        ]

    def shaped(dims, kind=jnp.float32):
        return jax.ShapeDtypeStruct(dims, kind)

    n = pieces + 1
    anywhere = pl.BlockSpec(memory_space=pl.ANY)
    vmem = pl.BlockSpec(memory_space=pltpu.VMEM)
    return pl.pallas_call(
        kernel,
        in_specs=[anywhere] * 11 + [vmem] * 4,
        out_specs=[anywhere] * 6 + [vmem],
        out_shape=[
            shaped((p_rows, D)),
            shaped((cont_len, D)),
            shaped((rows, 3 * D), jnp.bfloat16),
            shaped((rows, D), jnp.bfloat16),
            shaped((rows, ff), jnp.bfloat16),
            shaped((4 * rows, D), jnp.bfloat16),
            shaped((4, rows, s_width), jnp.bfloat16),
        ],
        scratch_shapes=[
            low(tokens, D), low(p_len, D), low(p_len, D), low(cont_len, D), low(cont_len, D),
            full(tokens, D), low(tokens, D), full(PAIR, tokens), low(tokens, D),
            low(p_len, D), low(p_len, D), low(cont_len, D), low(cont_len, D),
            low(2, 2, p_rows, D), low(2, p_rows, D), low(2, p_rows, D), low(3, D, D),
            full(tokens, D), low(3, 4, rows, D), full(16, s_width),
        ]
        + buffers(pieces, D)
        + [low(4, rows, s_width)]
        + buffers(1, s_width)
        + [
            sems(9), sems(n, 2), sems(n, 2), sems(n, 2), sems(n), sems(n), sems(n), sems(n),
            sems(n, 3), sems(n, 4), sems(n, 3), sems(n, 4), sems(n), sems(n), sems(n),
            sems(3), sems(4), sems(chunks, 2, 2), sems(chunks, 2, 2), sems(chunks, 2),
            sems(chunks, 2), sems(2),
        ],
        compiler_params=pltpu.CompilerParams(
            collective_id=2, has_side_effects=True, vmem_limit_bytes=VMEM_ALL
        ),
        name="finish",
    )(q, kp, vp, kc, vc, att, g_att, g9, g_resid, w_all, totals, lse, small, prompt, conts)


def place(g_prompt, g_conts, owned, summed, ff, classes):
    big = [g_prompt, g_conts, *owned]
    rows, across = summed.shape[1], D // 128

    def kernel(*refs):
        sources, fin = refs[:6], refs[6]
        targets, (o_bias, o_gain, o_in, o_stu, o_vec, o_pool, o_class, o_cb) = (
            refs[7:13],
            refs[13:21],
        )
        held, turned, sem_in, sem_out = refs[21:27], refs[27:31], refs[31], refs[32]
        reads = [
            pltpu.make_async_copy(sources[i], held[i], sem_in.at[i]) for i in (2, 4, 5, 3, 1, 0)
        ]
        for copy in reads:
            copy.start()

        def side(block):
            return fin[block, :, STU:].astype(jnp.float32)

        first = side(0)
        for i in range(8):
            target, at = (o_bias, i) if i < 6 else (o_gain, i - 6)
            for part in range(across):
                r = i * across + part
                target[at : at + 1, part * 128 : (part + 1) * 128] = first[r : r + 1, :]
        for part in range(ff // 128):
            r = 8 * across + part
            o_in[:, part * 128 : (part + 1) * 128] = first[r : r + 1, :]
        base = 8 * across + ff // 128
        o_vec[...] = first[base : base + 3, :]
        o_cb[...] = first[base + 3 : base + 4, :classes]
        every = jnp.concatenate([first, side(1)], 0)
        o_pool[...] = every[base + 8 : base + 8 + STU, :]
        o_class[...] = every[base + 8 + STU : base + 8 + 2 * STU, :classes]
        for block in range(4):
            o_stu[block * rows : (block + 1) * rows, :] = fin[block, :, :STU].astype(jnp.float32)
        writes = []
        for copy, i in zip(reads, (2, 4, 5, 3, 1, 0)):
            copy.wait()
            source = held[i]
            if i >= 2:
                source = turned[i - 2]
                source[...] = held[i][...].astype(jnp.float32)
            writes.append(pltpu.make_async_copy(source, targets[i], sem_out.at[i]))
            writes[-1].start()
        for copy in writes:
            copy.wait()

    def shaped(*dims):
        return jax.ShapeDtypeStruct(dims, jnp.float32)

    anywhere = pl.BlockSpec(memory_space=pl.ANY)
    vmem = pl.BlockSpec(memory_space=pltpu.VMEM)
    return pl.pallas_call(
        kernel,
        in_specs=[anywhere] * 6 + [vmem],
        out_specs=[anywhere] * 6 + [vmem] * 8,
        out_shape=[shaped(*part.shape) for part in big]
        + [
            shaped(6, D),
            shaped(2, D),
            shaped(1, ff),
            shaped(D, STU),
            shaped(3, STU),
            shaped(STU, STU),
            shaped(STU, classes),
            shaped(1, classes),
        ],
        scratch_shapes=[pltpu.VMEM(part.shape, part.dtype) for part in big]
        + [pltpu.VMEM(part.shape, jnp.float32) for part in owned]
        + [pltpu.SemaphoreType.DMA((6,)), pltpu.SemaphoreType.DMA((6,))],
        compiler_params=pltpu.CompilerParams(vmem_limit_bytes=VMEM_ALL),
        name="place",
    )(*big, summed)


def body(
    prompt,
    conts,
    prompt_cot,
    cont_cot,
    labels,
    w_qkv,
    w_out,
    w_in,
    w_ffo,
    layer_biases,
    norm_gains,
    bias_in,
    w_student,
    student_vectors,
    w_pool,
    w_class,
    bias_class,
):
    prompt_rows = prompt.shape[1]
    direct = (lax.axis_size("rep"), lax.axis_size("shard")) == (8, 4)
    project = project_and_attend if direct else project_native
    w_all, ffo_full, q, kp, vp, kc, vc, attended, log_totals = project(
        prompt[0], conts[0, 0], w_qkv, w_out, w_in, w_ffo, layer_biases
    )
    ahead = 3 if direct else 0
    out_p, out_c, logits, g9, g_resid, g_att, small, totals = middle(
        ahead,
        attended,
        prompt[0],
        conts[0, 0],
        prompt_cot[0],
        cont_cot[0, 0],
        labels,
        w_all,
        ffo_full if direct else ffo_full.reshape(-1, D, D),
        w_ffo,
        layer_biases,
        norm_gains,
        bias_in,
        w_student,
        student_vectors,
        w_pool,
        w_class,
        bias_class,
    )
    ff, classes = bias_in.shape[0], w_class.shape[1]
    if direct:
        outs = finish(
            ahead, totals, q, kp, vp, kc, vc, attended, log_totals, g_att, g9, g_resid, small, w_all,
            prompt[0], conts[0, 0], ff,
        )
        placed = place(outs[0], outs[1], outs[2:6], outs[6], ff, classes)
        g_prompt, g_conts, owned = placed[0], placed[1], placed[2:6]
        biases, gains_g, g_in, g_student, g_vectors, g_pool, g_class, g_cb = placed[6:]
    else:
        g_q, g_kp, g_vp, g_kc, g_vc = attend_backward(
            q, kp, vp, kc, vc, g_att, attended, log_totals, prompt_rows
        )
        tokens = jnp.concatenate([prompt[0], conts[0, 0]], 0)
        kv_sum = [
            lax.psum_scatter(part, "shard", scatter_dimension=0, tiled=True)
            for part in (g_kp, g_vp)
        ]
        g_k = jnp.concatenate([kv_sum[0], g_kc], 0)
        g_v = jnp.concatenate([kv_sum[1], g_vc], 0)
        g_tokens = g_resid
        for part, weight in ((g_k, w_all[0]), (g_v, w_all[1]), (g_q, w_all[2])):
            g_tokens = g_tokens + dot_second(part, weight)
        g_prompt, g_conts = g_tokens[:prompt_rows], g_tokens[prompt_rows:]
        g_qkvw = jnp.concatenate([dot_first(tokens, part) for part in (g_q, g_k, g_v)], 1)
        side = small[:, STU:]
        across = D // 128
        for at, part in ((0, g_q), (1, g_v)):
            total = jnp.sum(part.astype(jnp.float32), 0).reshape(across, 128)
            side = lax.dynamic_update_slice(side, total, (at * across, 0))
        small = jnp.concatenate([small[:, :STU], side], 1)
        owned, summed = sum_native(g9, g_qkvw, small)
        side = summed[:, STU:]
        base = 8 * across + ff // 128
        biases = side[: 6 * across].reshape(6, D)
        gains_g = side[6 * across : 8 * across].reshape(2, D)
        g_in = side[8 * across : base]
        g_student, g_vectors = summed[:, :STU], side[base : base + 3]
        g_pool = side[base + 8 : base + 8 + STU]
        g_class = side[base + 8 + STU : base + 8 + 2 * STU]
        g_cb = side[base + 3 : base + 4]
    return (
        out_p[None],
        out_c[None, None],
        logits[None],
        g_prompt[None],
        g_conts[None, None],
        *owned,
        biases,
        gains_g,
        g_in.reshape(ff),
        g_student,
        g_vectors,
        g_pool,
        g_class[:, :classes],
        g_cb[0, :classes],
    )


def solution(mesh):
    return jax.shard_map(
        body,
        mesh=mesh,
        in_specs=(
            P("rep", "shard", None),
            P("rep", "shard", None, None),
            P("rep", "shard", None),
            P("rep", "shard", None, None),
            P("rep", "shard"),
            P("shard", None),
            P("shard", None),
            P("shard", None),
            P("shard", None),
            P(),
            P(),
            P(),
            P(),
            P(),
            P(),
            P(),
            P(),
        ),
        out_specs=(
            P("rep", "shard", None),
            P("rep", "shard", None, None),
            P("rep", "shard", None),
            P("rep", "shard", None),
            P("rep", "shard", None, None),
            P("shard", None),
            P("shard", None),
            P("shard", None),
            P("shard", None),
            P(),
            P(),
            P(),
            P(),
            P(),
            P(),
            P(),
            P(),
        ),
        check_vma=False,
    )
```

profile of v0, /device:TPU:0, one launch (start us, length us, event | category | flops | bytes accessed | tf_op | source)
XLA Modules:
  0.0 252.8 jit_solution(9241097180833505232)
XLA Ops:
  1.3 0.0 copy-start.2
  1.3 0.0 copy-start.3
  1.3 69.3 %project_and_attend.1 = (bf16[8,4,192,768]{3,2,1,0:T(8,128)(2,1)}, bf16[4,3,192,768]{3,2,1,0:T(8,128)(2,1)}, bf16[768,768]{1,0:T(8,128)(2,1)}, bf16[512,768]{1,0...) custom-call(bf16[256,768]{1,0:T(8,128)(2,1)} %bitcast.20, ...), custom_call_target="tpu_custom_call" | custom-call | tf_op jit(solution)/shard_map/project_and_attend/pallas_call | solution.py:534
  70.6 0.0 copy-done.2
  70.6 0.1 copy.34
  70.7 0.6 pad.8.w_c
  71.4 0.0 copy-done.3
  71.4 0.5 pad.9.b_c
  71.9 56.0 %middle.1 = (bf16[256,768]{1,0:T(8,128)(2,1)}, bf16[512,768]{1,0:T(8,128)(2,1)}, f32[1,14]{1,0:T(1,128)}, bf16[9,768,768]{2,1,0:T(8,128)(2,1)}, f32[768,768]{1,0...) custom-call(s32[1,1]{1,0:T(1,128)S(6)} %copy.39.label_ref, ...), custom_call_target="tpu_custom_call" | custom-call | tf_op jit(solution)/shard_map/middle/pallas_call | solution.py:986
  127.9 114.3 %finish.1 = (f32[256,768]{1,0:T(8,128)}, f32[512,768]{1,0:T(8,128)}, bf16[192,2304]{1,0:T(8,128)(2,1)}, bf16[192,768]{1,0:T(8,128)(2,1)}, bf16[192,3072]{1,0:T(8...) custom-call(bf16[768,768]{1,0:T(8,128)(2,1)} %get-tuple-element.61.q_h, ...), custom_call_target="tpu_custom_call" | custom-call | tf_op jit(solution)/shard_map/finish/pallas_call | solution.py:1527
  242.2 0.0 copy-start.1
  242.2 0.0 copy-start
  242.2 7.0 %place.1 = (f32[256,768]{1,0:T(8,128)}, f32[512,768]{1,0:T(8,128)}, f32[192,2304]{1,0:T(8,128)}, f32[192,768]{1,0:T(8,128)}, f32[192,3072]{1,0:T(8,128)}, /*inde...) custom-call(f32[256,768]{1,0:T(8,128)} %get-tuple-element.72.refs_0_, ...), custom_call_target="tpu_custom_call" | custom-call | tf_op jit(solution)/shard_map/place/pallas_call | solution.py:1617
  249.2 0.0 copy-start.4
  249.2 1.5 copy.35
  250.7 0.0 copy-done.1
  250.7 0.7 copy.40
  251.4 0.0 copy-done
  251.4 0.9 copy.41
  252.3 0.0 copy-done.4
  252.3 0.5 copy.42
Async XLA Ops:
  1.3 69.3 %copy-start.2 = (f32[128,14]{0,1:T(8,128)S(1)}, f32[128,14]{0,1:T(8,128)}, u32[]{:S(2)}) copy-start(f32[128,14]{0,1:T(8,128)} %param.32) | copy-start | bytes 21508
  1.3 70.0 %copy-start.3 = (f32[14]{0:T(128)S(1)}, f32[14]{0:T(128)}, u32[]{:S(2)}) copy-start(f32[14]{0:T(128)} %param.33) | copy-start | bytes 172
  242.2 8.5 %copy-start.1 = (bf16[256,768]{1,0:T(8,128)(2,1)S(1)}, bf16[256,768]{1,0:T(8,128)(2,1)}, u32[]{:S(2)}) copy-start(bf16[256,768]{1,0:T(8,128)(2,1)} %get-tuple-element.58) | copy-start | bytes 1179652
  242.2 9.2 %copy-start = (bf16[512,768]{1,0:T(8,128)(2,1)S(1)}, bf16[512,768]{1,0:T(8,128)(2,1)}, u32[]{:S(2)}) copy-start(bf16[512,768]{1,0:T(8,128)(2,1)} %get-tuple-element.59) | copy-start | bytes 2359300
  249.2 3.2 %copy-start.4 = (f32[1,14]{1,0:T(1,128)S(1)}, f32[1,14]{1,0:T(1,128)}, u32[]{:S(2)}) copy-start(f32[1,14]{1,0:T(1,128)} %get-tuple-element.60) | copy-start | bytes 172
where the time goes:
time: 255 us; the launch traced here: 253 us
  Pallas kernels  247 us (97%)
  local copies, waits for them, and re-layouts  4.94 us (2%)
    pallas_call x1, Pallas kernels, finish(): pl.pallas_call(kernel, in_specs=[anywhere] * 11 + [vmem] * 4, out_specs=[...  114 us
    pallas_call x1, Pallas kernels, project_and_attend(): pl.pallas_call(kernel, in_specs=[vmem, vmem, anywhere, anywhere, anywhere...  69.3 us
    pallas_call x1, Pallas kernels, middle(): pl.pallas_call(kernel, in_specs=[pl.BlockSpec(memory_space=pltpu.SMEM), a...  56 us
    pallas_call x1, Pallas kernels, place(): pl.pallas_call(kernel, in_specs=[anywhere] * 6 + [vmem], out_specs=[anywh...  6.95 us

commit v1 on v0

--- a/solution.py
+++ b/solution.py
@@ -1,3 +1,5 @@
+import functools
+
 import jax
 import jax.numpy as jnp
 from jax import lax
@@ -240,8 +242,13 @@
 MESH_ID = pl.DeviceIdType.MESH
 
 
-def project_and_attend(prompt, conts, w_qkv, w_out, w_in, w_ffo, layer_biases):
-    pieces, early = 11, 4
+def project_and_attend(
+    prompt, conts, w_qkv, w_out, w_in, w_ffo, layer_biases, norm_gains, bias_in
+):
+    pieces, early = 12, 4
+    ff = bias_in.shape[0]
+    wide = D // TILE
+    inner_steps = ff // TILE
     by_z = (4, 5, 6, 7, 8, 9)
     rows = w_qkv.shape[0]
     p_rows, cont_len = prompt.shape[0], conts.shape[0]
@@ -249,15 +256,17 @@
     p_len = 4 * p_rows
     pairs = HEADS // 2
     tiles = tokens // TILE
+    steps = tokens // TILE
     chunk = 2 * PAIR
     chunks = D // chunk
     quarter = rows // 4
 
     def kernel(
-        xp, xc, wq, wo, wi, wf, bias, w_all_out, wf_out, q_out, kc_out, vc_out, kp_out, vp_out, att_out, lse,
-        stage, w_all, q, kc, vc, kp, vp, att,
+        xp, xc, wq, wo, wi, wf, bias, gain, b_in, w_all_out, wf_out, q_out, kc_out, vc_out, kp_out, vp_out, att_out,
+        norm_out, x1_out, act_out, slope_out, att_b_out, lse, rstd_out,
+        stage, w_all, q, kc, vc, kp, vp, att, norm1, x1_b, act, slope, att_b,
         load, c_s, c_r, x_s, x_r, y_s, y_r, z_s, z_r, d_s, d_r, e_s, e_r, w_sem,
-        kc_s, kc_r, kx_s, kx_r, kd_s, kd_r, out_sem,
+        kc_s, kc_r, kx_s, kx_r, kd_s, kd_r, out_sem, ff_sem, row_sem,
     ):
         rep, shard = lax.axis_index("rep"), lax.axis_index("shard")
         z, y = rep // 2, rep % 2
@@ -450,7 +459,7 @@
                 remote(kv_part(t, g, far), kd_s.at[g, t], kd_r.at[g, t], partner).wait_recv()
 
         serve_kv(0)
-        arrive = {4: 26.3, 5: 27.9, 6: 35.2, 7: 36.8, 8: 44.1, 9: 45.7, 10: 48.9}
+        arrive = {4: 26.3, 5: 27.9, 6: 35.2, 7: 36.8, 8: 44.1, 9: 45.7, 10: 48.9, 11: 52.1}
         work = [(33.6, serve_kv, 1), (42.4, serve_kv, 2), (27.0, serve_y, 3), (30.0, complete, 3)]
         for k in range(4, pieces):
             at = arrive[k]
@@ -460,8 +469,10 @@
             else:
                 work += [(at + 6, serve_y, k), (at + 9, complete, k)]
         slots = pairs * tiles
-        work = [(max(0, round((at - 26) / 1.37 - 0.6)), act, k) for at, act, k in work]
         work.sort(key=lambda item: item[0])
+        later = [item for item in work if item[0] > 26 + 1.37 * slots]
+        work = [(max(0, round((at - 26) / 1.37 - 0.6)), job, k) for at, job, k in work if at <= 26 + 1.37 * slots]
+        work = [(min(slot, slots - 1), job, k) for slot, job, k in work]
 
         def att_store(p):
             lanes = pl.ds(pl.multiple_of(p * PAIR, PAIR), PAIR)
@@ -500,9 +511,74 @@
         kept += [(kp, kp_out, 3), (vp, vp_out, 4)]
         for item in kept[3:]:
             keep(*item).start()
-        for slot, action, k in work:
-            if slot >= slots:
-                action(k)
+
+        def row(i):
+            return pl.ds(pl.multiple_of(i * TILE, TILE), TILE)
+
+        def row_stores(i):
+            pairs_of = [(norm1, norm_out), (x1_b, x1_out), (att_b, att_b_out)]
+            return [
+                pltpu.make_async_copy(ref.at[row(i), :], out.at[row(i), :], row_sem.at[n, i])
+                for n, (ref, out) in enumerate(pairs_of)
+            ]
+
+        def normalized(i, carry):
+            part = att[row(i), :].astype(jnp.bfloat16)
+            att_b[row(i), :] = part
+            values = dot_plain(part, weight(3)) + bias[2:3, :] + norm1[row(i), :]
+            center = values - jnp.mean(values, -1, keepdims=True)
+            spread = jnp.mean(center * center, -1, keepdims=True)
+            scale = lax.rsqrt(spread + 1e-05)
+            hat = center * scale
+            norm1[row(i), :] = hat
+            rstd_out[row(i), :] = jnp.broadcast_to(scale, (TILE, 128))
+            x1_b[row(i), :] = (hat * gain[0:1, :] + bias[4:5, :]).astype(jnp.bfloat16)
+            for copy in row_stores(i):
+                copy.start()
+            return carry
+
+        norm1[:p_rows, :] = xp[...].astype(jnp.float32)
+        norm1[p_rows:, :] = xc[...].astype(jnp.float32)
+        lax.fori_loop(0, steps, normalized, 0)
+
+        def ff_stores(i):
+            columns = pl.ds(pl.multiple_of(i * TILE, TILE), TILE)
+            return [
+                pltpu.make_async_copy(ref.at[:, columns], out.at[:, columns], ff_sem.at[n, i])
+                for n, (ref, out) in enumerate([(act, act_out), (slope, slope_out)])
+            ]
+
+        def inner(i, carry):
+            lanes = pl.ds(pl.multiple_of(lax.rem(i, wide) * TILE, TILE), TILE)
+            columns = pl.ds(pl.multiple_of(i * TILE, TILE), TILE)
+            block = w_all[4 + i // wide, :, :, lanes].reshape(D, TILE)
+            hidden = dot_plain(x1_b[...], block) + b_in[:, columns]
+            cdf = 0.5 * (1.0 + lax.erf(hidden * 2.0 ** (-0.5)))
+            act[:, columns] = (hidden * cdf).astype(jnp.bfloat16)
+            density = jnp.exp(hidden * hidden * (-0.5)) * 0.3989422804014327
+            slope[:, columns] = (cdf + hidden * density).astype(jnp.bfloat16)
+            for copy in ff_stores(i):
+                copy.start()
+            for at, job, k in later:
+                step = min(max(0, round((at - 54.5) / 0.73 - 0.5)), inner_steps - 1)
+                pl.when(i == step)(functools.partial(job, k))
+            return carry
+
+        lax.fori_loop(0, inner_steps, inner, 0)
+
+        def ff_wait(i, carry):
+            for copy in ff_stores(i):
+                copy.wait()
+            return carry
+
+        lax.fori_loop(0, inner_steps, ff_wait, 0)
+
+        def row_wait(i, carry):
+            for copy in row_stores(i):
+                copy.wait()
+            return carry
+
+        lax.fori_loop(0, steps, row_wait, 0)
         for item in kept:
             keep(*item).wait()
 
@@ -533,18 +609,24 @@
     n = pieces
     out = pl.pallas_call(
         kernel,
-        in_specs=[vmem, vmem, anywhere, anywhere, anywhere, anywhere, vmem],
-        out_specs=[anywhere] * 8 + [vmem],
+        in_specs=[vmem, vmem, anywhere, anywhere, anywhere, anywhere, vmem, vmem, vmem],
+        out_specs=[anywhere] * 13 + [vmem] * 2,
         out_shape=[
             low(8, 4, rows, D),
-            low(4, 3, rows, D),
+            low(4, 4, rows, D),
             low(tokens, D),
             low(cont_len, D),
             low(cont_len, D),
             low(p_len, D),
             low(p_len, D),
             jax.ShapeDtypeStruct((tokens, D), jnp.float32),
+            jax.ShapeDtypeStruct((tokens, D), jnp.float32),
+            low(tokens, D),
+            low(tokens, ff),
+            low(tokens, ff),
+            low(tokens, D),
             jax.ShapeDtypeStruct((pairs, 8, tokens), jnp.float32),
+            jax.ShapeDtypeStruct((tokens, 128), jnp.float32),
         ],
         scratch_shapes=[
             pltpu.VMEM((n, rows, D), jnp.float32),
@@ -555,21 +637,29 @@
             pltpu.VMEM((p_len, D), jnp.bfloat16),
             pltpu.VMEM((p_len, D), jnp.bfloat16),
             pltpu.VMEM((tokens, D), jnp.float32),
+            pltpu.VMEM((tokens, D), jnp.float32),
+            pltpu.VMEM((tokens, D), jnp.bfloat16),
+            pltpu.VMEM((tokens, ff), jnp.bfloat16),
+            pltpu.VMEM((tokens, ff), jnp.bfloat16),
+            pltpu.VMEM((tokens, D), jnp.bfloat16),
         ]
         + [sems(n)] * 14
         + [sems(chunks, 2)] * 6
-        + [sems(5 + pairs)],
+        + [sems(5 + pairs), sems(2, inner_steps), sems(3, steps)],
         compiler_params=pltpu.CompilerParams(
             collective_id=1, has_side_effects=True, vmem_limit_bytes=VMEM_ALL
         ),
         name="project_and_attend",
-    )(prompt, conts, w_qkv, w_out, w_in, w_ffo, layer_biases)
-    w_all, wf, q, kc, vc, kp, vp, att, lse = out
+    )(prompt, conts, w_qkv, w_out, w_in, w_ffo, layer_biases, norm_gains, bias_in[None])
+    w_all, wf, q, kc, vc, kp, vp, att, norm1, x1_b, act, slope, att_b, lse, rstd1 = out
     w_all = w_all.reshape(8, 4 * rows, D)
-    return w_all, wf.reshape(4, 3 * rows, D), q, kp, vp, kc, vc, att, lse
-
-
-def project_native(prompt, conts, w_qkv, w_out, w_in, w_ffo, layer_biases):
+    wf = wf.reshape(4, 4 * rows, D)
+    return w_all, wf, q, kp, vp, kc, vc, att, lse, (norm1, rstd1, x1_b, act, slope, att_b)
+
+
+def project_native(
+    prompt, conts, w_qkv, w_out, w_in, w_ffo, layer_biases, norm_gains, bias_in
+):
     rows = prompt.shape[0]
 
     def gathered(value):
@@ -585,7 +675,21 @@
     att, lse = attend_forward(q, kp, vp, kc, vc, rows)
     blocks = [qkv[:, D : 2 * D], qkv[:, 2 * D :], qkv[:, :D], out]
     blocks += [inner[:, i * D : (i + 1) * D] for i in range(inner.shape[1] // D)]
-    return jnp.stack(blocks), ffo, q, kp, vp, kc, vc, att, lse
+    att_b = att.astype(jnp.bfloat16)
+    values = tokens.astype(jnp.float32) + dot_plain(att_b, out) + layer_biases[2]
+    center = values - jnp.mean(values, -1, keepdims=True)
+    scale = lax.rsqrt(jnp.mean(center * center, -1, keepdims=True) + 1e-05)
+    norm1 = center * scale
+    x1_b = (norm1 * norm_gains[0] + layer_biases[4]).astype(jnp.bfloat16)
+    hidden = dot_plain(x1_b, inner) + bias_in
+    cdf = 0.5 * (1.0 + lax.erf(hidden * 2.0 ** (-0.5)))
+    density = jnp.exp(hidden * hidden * (-0.5)) * 0.3989422804014327
+    act = (hidden * cdf).astype(jnp.bfloat16)
+    slope = (cdf + hidden * density).astype(jnp.bfloat16)
+    rstd1 = jnp.broadcast_to(scale, (tokens.shape[0], 128))
+    state = (norm1, rstd1, x1_b, act, slope, att_b)
+    ffo = ffo.reshape(-1, D, D)
+    return jnp.stack(blocks), ffo, q, kp, vp, kc, vc, att, lse, state
 
 
 def student_head(label, stu, vectors, w_pool, w_class, bias_class, classes):
@@ -622,12 +726,12 @@
 
     top = jnp.tanh(times(pooled, w_pool) + bias_pool)
     lane = lax.broadcasted_iota(jnp.int32, (1, STU), 1)
-    logits = times(top, w_class) + bias_class
+    logits = times_turned(top, w_class) + bias_class
     seen = jnp.where(lane < classes, logits, NEG_BIG)
     expo_l = jnp.exp(seen - jnp.max(seen, 1, keepdims=True))
     g_logits = expo_l / jnp.sum(expo_l, 1, keepdims=True) - jnp.where(lane == label, 1.0, 0.0)
-    g_class = column(top) * g_logits
-    g_pre = times_turned(g_logits, w_class) * (1.0 - top * top)
+    g_class = column(g_logits) * top
+    g_pre = times(g_logits, w_class) * (1.0 - top * top)
     g_pool = column(pooled) * g_pre
     g_pooled = times_turned(g_pre, w_pool)
     g_weights = by_head(stu * g_pooled)
@@ -639,57 +743,52 @@
 
 
 def middle(
-    ahead, att, prompt, conts, prompt_cot, cont_cot, labels, w_all, wf, wf_rows,
+    ahead, state, prompt_cot, cont_cot, labels, w_all, wf,
     biases, gains, bias_in, student, vectors, w_pool, w_class, bias_class,
 ):
-    p_rows, cont_len = prompt.shape[0], conts.shape[0]
+    p_rows, cont_len = prompt_cot.shape[0], cont_cot.shape[0]
     tokens = p_rows + cont_len
     ff = bias_in.shape[0]
     blocks = ff // D
     steps = tokens // TILE
     wide = D // TILE
     classes = w_class.shape[1]
-    w_class_p = jnp.pad(w_class, ((0, 0), (0, STU - classes)))
-    bias_class_p = jnp.pad(bias_class[None], ((0, 0), (0, STU - classes)))
     g_names = 2 * blocks + 1
 
     def kernel(
-        label_ref, att_h, xp, xc, cp, cc, w_h, wf_h, wf_own, bias, gain, b_in, w_stu, vec, w_p, w_c, b_c,
+        label_ref, norm_h, rstd_h, x1_h, act_h, slope_h, att_b_h, cp, cc, w_h, wf_h, bias, gain, w_stu, vec, w_p, w_c, b_c,
         out_p, out_c, logits_out, grads_h, g_r1_h, g_att_h, small, totals_h,
-        x_v, cot_v, out_v, att_v, att_b, w_v, wf_v, norm1, norm2, rstd1, rstd2, x1_b, act, slope, g_res, g_ffn, g_br, g_stu_b, grads,
+        cot_v, out_v, w_c_v, b_c_v, att_b, w_v, wf_v, norm1, norm2, rstd1, rstd2, x1_b, act, slope, g_res, g_ffn, g_br, g_stu_b, grads,
         sums, in_sum, load, store, *links,
     ):
         def fetch(source, target, i):
             return pltpu.make_async_copy(source, target, load.at[i])
 
         loads = [
-            fetch(att_h, att_v, 0),
-            fetch(w_h.at[3], w_v.at[0], 1),
-            fetch(w_h.at[pl.ds(4, blocks)], w_v.at[pl.ds(1, blocks)], 2),
-            fetch(wf_h, wf_v.at[:, : wf_h.shape[1]], 3),
-            fetch(xp, x_v.at[:p_rows], 4),
-            fetch(xc, x_v.at[p_rows:], 5),
-            fetch(cp, cot_v.at[:p_rows], 6),
-            fetch(cc, cot_v.at[p_rows:], 7),
+            fetch(act_h, act, 0),
+            fetch(wf_h, wf_v, 1),
+            fetch(norm_h, norm1, 2),
+            fetch(cp, cot_v.at[:p_rows], 3),
+            fetch(cc, cot_v.at[p_rows:], 4),
+            fetch(slope_h, slope, 5),
+            fetch(x1_h, x1_b, 6),
+            fetch(rstd_h, rstd1, 7),
+            fetch(w_h.at[pl.ds(3, 1 + blocks)], w_v, 8),
+            fetch(att_b_h, att_b, 9),
         ]
         for copy in loads:
             copy.start()
         rows = D // blocks
         if ahead:
-            (stage, cr, xr, w_s, w_r, c_s, c_r, x_s, x_r) = links
-            own_rows = fetch(wf_own.at[pl.ds(D - rows, rows), :], stage, 8)
-            own_rows.start()
+            (cr, xr, c_s, c_r, x_s, x_r) = links
             rep, shard = lax.axis_index("rep"), lax.axis_index("shard")
-            z, y = rep // 2, rep % 2
             x, core = shard // 2, shard % 2
             partner = (rep, 2 * x + 1 - core)
             across = (rep, 2 * (1 - x) + core)
-            beside = (2 * z + 1 - y, shard)
-            there, far = 2 * (1 - x) + core, 2 * (1 - x) + 1 - core
             barrier = pltpu.get_barrier_semaphore()
-            for other in (partner, across, beside):
+            for other in (partner, across):
                 pl.semaphore_signal(barrier, inc=1, device_id=other, device_id_type=MESH_ID)
-            pl.semaphore_wait(barrier, 3)
+            pl.semaphore_wait(barrier, 2)
 
             def remote(source, target, send, recv, device):
                 return pltpu.make_async_remote_copy(
@@ -701,15 +800,6 @@
                     device_id_type=MESH_ID,
                 )
 
-            def moved(i, block, which, device):
-                first = D - rows
-                at = pl.ds(first, rows)
-                if which is not None:
-                    half = rows // 2
-                    at = pl.ds(pl.multiple_of(first + which * half, 16), half)
-                ref = wf_v.at[block, at, :]
-                return remote(ref, ref, w_s.at[i], w_r.at[i], device)
-
             def core_copy(k, xx):
                 block = pl.ds(pl.multiple_of((2 * xx + 1 - core) * rows, 16), rows)
                 return remote(
@@ -721,25 +811,6 @@
 
             def x_copy(k):
                 return remote(grads.at[k, mine(1 - x), :], xr.at[k], x_s.at[k], x_r.at[k], across)
-
-            own_rows.wait()
-            wf_v[shard, D - rows :, :] = stage[...].astype(jnp.bfloat16)
-            moved(1, shard, y, across).start()
-            moved(0, shard, None, partner).start()
-
-        def serve_across():
-            moved(1, there, y, across).wait_recv()
-            moved(2, there, y, beside).start()
-            moved(3, there, y, partner).start()
-
-        def serve_beside():
-            moved(2, there, 1 - y, beside).wait_recv()
-            moved(4, there, 1 - y, partner).start()
-
-        def gathered():
-            moved(0, 2 * x + 1 - core, None, partner).wait_recv()
-            moved(3, far, y, partner).wait_recv()
-            moved(4, far, 1 - y, partner).wait_recv()
 
         def stage_x():
             for k in range(ahead):
@@ -783,38 +854,8 @@
         def add_sum(i, values):
             sums[i : i + 1, :] += jnp.sum(values, 0, keepdims=True)
 
-        for i in (0, 1, 4, 5):
+        for i in range(3):
             loads[i].wait()
-
-        @loop(steps)
-        def _(i):
-            part = att_v[row(i), :].astype(jnp.bfloat16)
-            att_b[row(i), :] = part
-            branch = dot_plain(part, w_v[0]) + bias[2:3, :]
-            hat, scale = normalize(x_v[row(i), :].astype(jnp.float32) + branch)
-            norm1[row(i), :] = hat
-            rstd1[row(i), :] = jnp.broadcast_to(scale, (TILE, 128))
-            x1_b[row(i), :] = (hat * gain[0:1, :] + bias[4:5, :]).astype(jnp.bfloat16)
-
-        loads[2].wait()
-
-        def inner(i, carry):
-            lanes = pl.ds(pl.multiple_of(lax.rem(i, wide) * TILE, TILE), TILE)
-            columns = pl.ds(pl.multiple_of(i * TILE, TILE), TILE)
-            hidden = dot_plain(x1_b[...], w_v[1 + i // wide, :, lanes]) + b_in[:, columns]
-            cdf = 0.5 * (1.0 + lax.erf(hidden * 2.0 ** (-0.5)))
-            act[:, columns] = (hidden * cdf).astype(jnp.bfloat16)
-            density = jnp.exp(hidden * hidden * (-0.5)) * 0.3989422804014327
-            slope[:, columns] = (cdf + hidden * density).astype(jnp.bfloat16)
-            if ahead:
-                pl.when(i == 3)(serve_across)
-                pl.when(i == 10)(serve_beside)
-            return carry
-
-        lax.fori_loop(0, ff // TILE, inner, 0)
-        loads[3].wait()
-        if ahead:
-            gathered()
 
         @loop(steps)
         def _(i):
@@ -836,11 +877,16 @@
         base = 8 * (D // 128) + ff // 128
         w_stu_b = w_stu[...].astype(jnp.bfloat16)
 
+        w_c_v[...] = jnp.zeros_like(w_c_v)
+        b_c_v[...] = jnp.zeros_like(b_c_v)
+        w_c_v[:classes, :] = w_c[...]
+        b_c_v[:1, :classes] = b_c[...]
+
         @pl.when(lax.axis_index("rep") >= 0)
         def _():
             stu = dot_plain(out_v[p_rows:, :], w_stu_b) + vec[0:1, :]
             logits, g_stu, g_query, g_pre, g_pool, g_class, g_logits = student_head(
-                label_ref[0, 0], stu, vec, w_p[...], w_c[...], b_c[...], classes
+                label_ref[0, 0], stu, vec, w_p[...], w_c_v[...], b_c_v[:1, :], classes
             )
             logits_out[...] = logits[:, :classes]
             low = g_stu.astype(jnp.bfloat16)
@@ -851,11 +897,11 @@
             small[base + 2 : base + 3, STU:] = g_pre
             small[base + 3 : base + 4, STU:] = g_logits
             small[base + 8 : base + 8 + STU, STU:] = g_pool
-            small[base + 8 + STU : base + 8 + 2 * STU, STU:] = g_class
+            small[base + 8 + STU : base + 24 + STU, STU:] = g_class[:16]
 
         small[:, :STU] = dot_first(out_v[p_rows:, :], g_stu_b[p_rows:, :])
-        loads[6].wait()
-        loads[7].wait()
+        for i in range(3, 10):
+            loads[i].wait()
 
         @loop(steps)
         def _(i):
@@ -953,12 +999,6 @@
             for xx in range(2):
                 core_copy(k, xx).wait_send()
             x_copy(k).wait_send()
-        if ahead:
-            moved(0, shard, None, partner).wait_send()
-            moved(1, shard, y, across).wait_send()
-            moved(2, there, y, beside).wait_send()
-            moved(3, there, y, partner).wait_send()
-            moved(4, there, 1 - y, partner).wait_send()
 
     anywhere = pl.BlockSpec(memory_space=pl.ANY)
     vmem = pl.BlockSpec(memory_space=pltpu.VMEM)
@@ -975,19 +1015,15 @@
         )
         piece = (D // blocks, D)
         link_scratch = [
-            pltpu.VMEM(piece, jnp.float32),
             pltpu.VMEM((ahead, 2, *piece), low),
             pltpu.VMEM((ahead, *piece), low),
         ]
-        link_scratch += [pltpu.SemaphoreType.DMA((5,))] * 2
         link_scratch += [pltpu.SemaphoreType.DMA((ahead, 2))] * 2
         link_scratch += [pltpu.SemaphoreType.DMA((ahead,))] * 2
 
     return pl.pallas_call(
         kernel,
-        in_specs=[pl.BlockSpec(memory_space=pltpu.SMEM), anywhere]
-        + [anywhere] * 7
-        + [vmem] * 8,
+        in_specs=[pl.BlockSpec(memory_space=pltpu.SMEM)] + [anywhere] * 10 + [vmem] * 7,
         out_specs=[anywhere, anywhere, vmem, anywhere, anywhere, anywhere, vmem, anywhere],
         out_shape=[
             shaped((p_rows, D), low),
@@ -1002,8 +1038,8 @@
         scratch_shapes=[
             pltpu.VMEM((tokens, D), low),
             pltpu.VMEM((tokens, D), low),
-            pltpu.VMEM((tokens, D), low),
-            pltpu.VMEM((tokens, D), jnp.float32),
+            pltpu.VMEM((STU, STU), jnp.float32),
+            pltpu.VMEM((8, STU), jnp.float32),
             pltpu.VMEM((tokens, D), low),
             pltpu.VMEM((1 + blocks, D, D), low),
             pltpu.VMEM((blocks, D, D), low),
@@ -1021,7 +1057,7 @@
             pltpu.VMEM((g_names, D, D), low),
             pltpu.VMEM((8, D), jnp.float32),
             pltpu.VMEM((1, ff), jnp.float32),
-            pltpu.SemaphoreType.DMA((9,)),
+            pltpu.SemaphoreType.DMA((10,)),
             pltpu.SemaphoreType.DMA((g_names + 4,)),
         ]
         + link_scratch,
@@ -1029,22 +1065,18 @@
         name="middle",
     )(
         labels,
-        att,
-        prompt,
-        conts,
+        *state,
         prompt_cot,
         cont_cot,
         w_all,
         wf,
-        wf_rows,
         biases,
         gains,
-        bias_in[None],
         student,
         vectors,
         w_pool,
-        w_class_p,
-        bias_class_p,
+        w_class.T,
+        bias_class[None],
     )
 
 
@@ -1560,20 +1592,20 @@
     )(q, kp, vp, kc, vc, att, g_att, g9, g_resid, w_all, totals, lse, small, prompt, conts)
 
 
-def place(g_prompt, g_conts, owned, summed, ff, classes):
-    big = [g_prompt, g_conts, *owned]
+def place(g_prompt, g_conts, owned, out_p, out_c, logits, summed, ff, classes):
+    big = [g_prompt, g_conts, *owned, out_p, out_c]
+    count = len(big)
+    order = (2, 4, 5, 3, 1, 0, 7, 6)
     rows, across = summed.shape[1], D // 128
 
     def kernel(*refs):
-        sources, fin = refs[:6], refs[6]
-        targets, (o_bias, o_gain, o_in, o_stu, o_vec, o_pool, o_class, o_cb) = (
-            refs[7:13],
-            refs[13:21],
-        )
-        held, turned, sem_in, sem_out = refs[21:27], refs[27:31], refs[31], refs[32]
-        reads = [
-            pltpu.make_async_copy(sources[i], held[i], sem_in.at[i]) for i in (2, 4, 5, 3, 1, 0)
-        ]
+        sources, fin, logits_in = refs[:count], refs[count], refs[count + 1]
+        outs = refs[count + 2 :]
+        targets = outs[:count]
+        o_bias, o_gain, o_in, o_stu, o_vec, o_pool, o_class, o_cb, o_logits = outs[count : count + 9]
+        scratch = outs[count + 9 :]
+        held, turned, (sem_in, sem_out) = scratch[:count], scratch[count:-2], scratch[-2:]
+        reads = [pltpu.make_async_copy(sources[i], held[i], sem_in.at[i]) for i in order]
         for copy in reads:
             copy.start()
 
@@ -1594,14 +1626,15 @@
         o_cb[...] = first[base + 3 : base + 4, :classes]
         every = jnp.concatenate([first, side(1)], 0)
         o_pool[...] = every[base + 8 : base + 8 + STU, :]
-        o_class[...] = every[base + 8 + STU : base + 8 + 2 * STU, :classes]
+        o_class[...] = every[base + 8 + STU : base + 8 + STU + classes, :]
         for block in range(4):
             o_stu[block * rows : (block + 1) * rows, :] = fin[block, :, :STU].astype(jnp.float32)
         writes = []
-        for copy, i in zip(reads, (2, 4, 5, 3, 1, 0)):
+        o_logits[...] = logits_in[...]
+        for copy, i in zip(reads, order):
             copy.wait()
             source = held[i]
-            if i >= 2:
+            if 2 <= i < 6:
                 source = turned[i - 2]
                 source[...] = held[i][...].astype(jnp.float32)
             writes.append(pltpu.make_async_copy(source, targets[i], sem_out.at[i]))
@@ -1616,9 +1649,10 @@
     vmem = pl.BlockSpec(memory_space=pltpu.VMEM)
     return pl.pallas_call(
         kernel,
-        in_specs=[anywhere] * 6 + [vmem],
-        out_specs=[anywhere] * 6 + [vmem] * 8,
-        out_shape=[shaped(*part.shape) for part in big]
+        in_specs=[anywhere] * count + [vmem] * 2,
+        out_specs=[anywhere] * count + [vmem] * 9,
+        out_shape=[shaped(*part.shape) for part in big[:6]]
+        + [jax.ShapeDtypeStruct(part.shape, part.dtype) for part in big[6:]]
         + [
             shaped(6, D),
             shaped(2, D),
@@ -1626,15 +1660,16 @@
             shaped(D, STU),
             shaped(3, STU),
             shaped(STU, STU),
-            shaped(STU, classes),
+            shaped(classes, STU),
+            shaped(1, classes),
             shaped(1, classes),
         ],
         scratch_shapes=[pltpu.VMEM(part.shape, part.dtype) for part in big]
         + [pltpu.VMEM(part.shape, jnp.float32) for part in owned]
-        + [pltpu.SemaphoreType.DMA((6,)), pltpu.SemaphoreType.DMA((6,))],
+        + [pltpu.SemaphoreType.DMA((count,)), pltpu.SemaphoreType.DMA((count,))],
         compiler_params=pltpu.CompilerParams(vmem_limit_bytes=VMEM_ALL),
         name="place",
-    )(*big, summed)
+    )(*big, summed, logits)
 
 
 def body(
@@ -1659,21 +1694,18 @@
     prompt_rows = prompt.shape[1]
     direct = (lax.axis_size("rep"), lax.axis_size("shard")) == (8, 4)
     project = project_and_attend if direct else project_native
-    w_all, ffo_full, q, kp, vp, kc, vc, attended, log_totals = project(
-        prompt[0], conts[0, 0], w_qkv, w_out, w_in, w_ffo, layer_biases
+    w_all, ffo_full, q, kp, vp, kc, vc, attended, log_totals, state = project(
+        prompt[0], conts[0, 0], w_qkv, w_out, w_in, w_ffo, layer_biases, norm_gains, bias_in
     )
     ahead = 3 if direct else 0
     out_p, out_c, logits, g9, g_resid, g_att, small, totals = middle(
         ahead,
-        attended,
-        prompt[0],
-        conts[0, 0],
+        state,
         prompt_cot[0],
         cont_cot[0, 0],
         labels,
         w_all,
-        ffo_full if direct else ffo_full.reshape(-1, D, D),
-        w_ffo,
+        ffo_full,
         layer_biases,
         norm_gains,
         bias_in,
@@ -1689,9 +1721,9 @@
             ahead, totals, q, kp, vp, kc, vc, attended, log_totals, g_att, g9, g_resid, small, w_all,
             prompt[0], conts[0, 0], ff,
         )
-        placed = place(outs[0], outs[1], outs[2:6], outs[6], ff, classes)
-        g_prompt, g_conts, owned = placed[0], placed[1], placed[2:6]
-        biases, gains_g, g_in, g_student, g_vectors, g_pool, g_class, g_cb = placed[6:]
+        placed = place(outs[0], outs[1], outs[2:6], out_p, out_c, logits, outs[6], ff, classes)
+        g_prompt, g_conts, owned, out_p, out_c = placed[0], placed[1], placed[2:6], *placed[6:8]
+        biases, gains_g, g_in, g_student, g_vectors, g_pool, g_class, g_cb, logits = placed[8:]
     else:
         g_q, g_kp, g_vp, g_kc, g_vc = attend_backward(
             q, kp, vp, kc, vc, g_att, attended, log_totals, prompt_rows
@@ -1722,7 +1754,7 @@
         g_in = side[8 * across : base]
         g_student, g_vectors = summed[:, :STU], side[base : base + 3]
         g_pool = side[base + 8 : base + 8 + STU]
-        g_class = side[base + 8 + STU : base + 8 + 2 * STU]
+        g_class = side[base + 8 + STU : base + 8 + STU + classes]
         g_cb = side[base + 3 : base + 4]
     return (
         out_p[None],
@@ -1737,7 +1769,7 @@
         g_student,
         g_vectors,
         g_pool,
-        g_class[:, :classes],
+        g_class.T,
         g_cb[0, :classes],
     )
 

time: 255 us -> 245 us (0.961)
  Pallas kernels: 247 us -> 242 us
  local copies, waits for them, and re-layouts: 4.94 us -> 0 us
    pallas_call x2, Pallas kernels: 63 us -> 52 us  [the longest x1 44.3 us: middle(): pl.pallas_call(kernel, in_specs=[pl.BlockSpec(memory_space=pltpu.SMEM)] +...]
    pallas_call x1, Pallas kernels: 69.3 us -> 75.6 us  [project_and_attend(): pl.pallas_call(kernel, in_specs=[vmem, vmem, anywhere, anywhere, anywhere...]
    unnamed x15 -> x0, local copies, waits for them, and re-layouts: 3.78 us -> none
where the time goes in v1:
time: 245 us; the launch traced here: 243 us
  Pallas kernels  242 us (99%)
    pallas_call x1, Pallas kernels, finish(): pl.pallas_call(kernel, in_specs=[anywhere] * 11 + [vmem] * 4, out_specs=[...  114 us
    pallas_call x1, Pallas kernels, project_and_attend(): pl.pallas_call(kernel, in_specs=[vmem, vmem, anywhere, anywhere, anywhere...  75.6 us
    pallas_call x1, Pallas kernels, middle(): pl.pallas_call(kernel, in_specs=[pl.BlockSpec(memory_space=pltpu.SMEM)] +...  44.3 us
    pallas_call x1, Pallas kernels, place(): pl.pallas_call(kernel, in_specs=[anywhere] * count + [vmem] * 2, out_spec...  7.65 us

profile of v1, /device:TPU:0, one launch (start us, length us, event | category | flops | bytes accessed | tf_op | source)
XLA Modules:
  0.0 243.3 jit_solution(17833971856473213543)
XLA Ops:
  1.3 75.6 %project_and_attend.1 = (bf16[8,4,192,768]{3,2,1,0:T(8,128)(2,1)}, bf16[4,4,192,768]{3,2,1,0:T(8,128)(2,1)}, bf16[768,768]{1,0:T(8,128)(2,1)}, bf16[512,768]{1,0...) custom-call(bf16[256,768]{1,0:T(8,128)(2,1)} %bitcast.22, ...), custom_call_target="tpu_custom_call" | custom-call | tf_op jit(solution)/shard_map/project_and_attend/pallas_call | solution.py:610
  76.9 44.3 %middle.1 = (bf16[256,768]{1,0:T(8,128)(2,1)}, bf16[512,768]{1,0:T(8,128)(2,1)}, f32[1,14]{1,0:T(1,128)}, bf16[9,768,768]{2,1,0:T(8,128)(2,1)}, f32[768,768]{1,0...) custom-call(s32[1,1]{1,0:T(1,128)S(6)} %copy.34.label_ref, ...), custom_call_target="tpu_custom_call" | custom-call | tf_op jit(solution)/shard_map/middle/pallas_call | solution.py:1024
  121.2 114.3 %finish.1 = (f32[256,768]{1,0:T(8,128)}, f32[512,768]{1,0:T(8,128)}, bf16[192,2304]{1,0:T(8,128)(2,1)}, bf16[192,768]{1,0:T(8,128)(2,1)}, bf16[192,3072]{1,0:T(8...) custom-call(bf16[768,768]{1,0:T(8,128)(2,1)} %get-tuple-element.64.q_h, ...), custom_call_target="tpu_custom_call" | custom-call | tf_op jit(solution)/shard_map/finish/pallas_call | solution.py:1559
  235.5 7.7 %place.1 = (f32[256,768]{1,0:T(8,128)}, f32[512,768]{1,0:T(8,128)}, f32[192,2304]{1,0:T(8,128)}, f32[192,768]{1,0:T(8,128)}, f32[192,3072]{1,0:T(8,128)}, /*inde...) custom-call(f32[256,768]{1,0:T(8,128)} %get-tuple-element.84.refs_0_, ...), custom_call_target="tpu_custom_call" | custom-call | tf_op jit(solution)/shard_map/place/pallas_call | solution.py:1650

commit v2 on v1

--- a/solution.py
+++ b/solution.py
@@ -257,7 +257,7 @@
     pairs = HEADS // 2
     tiles = tokens // TILE
     steps = tokens // TILE
-    chunk = 2 * PAIR
+    chunk = PAIR
     chunks = D // chunk
     quarter = rows // 4
 
@@ -429,9 +429,10 @@
             for t in range(2):
                 kv_across(t, g).start()
                 kv_core(t, g).start()
-            for k in waiting[: 2 if g < chunks - 1 else pieces]:
+            sent = 0 if g == 0 else 1 if g < chunks - 1 else pieces
+            for k in waiting[:sent]:
                 send_piece(k)
-            waiting = waiting[2:]
+            waiting = waiting[sent:]
         vc[...] = (dot_plain(xc[...], weight(1)) + bias[1:2, :]).astype(jnp.bfloat16)
         serve_y(2)
         serve_x(3)
@@ -459,8 +460,10 @@
                 remote(kv_part(t, g, far), kd_s.at[g, t], kd_r.at[g, t], partner).wait_recv()
 
         serve_kv(0)
-        arrive = {4: 26.3, 5: 27.9, 6: 35.2, 7: 36.8, 8: 44.1, 9: 45.7, 10: 48.9, 11: 52.1}
-        work = [(33.6, serve_kv, 1), (42.4, serve_kv, 2), (27.0, serve_y, 3), (30.0, complete, 3)]
+        arrive = {4: 26.2, 5: 30.6, 6: 35.1, 7: 39.5, 8: 43.9, 9: 45.5, 10: 48.7, 11: 51.9}
+        work = [(27.0, serve_y, 3), (30.0, complete, 3)]
+        forward = (27.0, 31.1, 35.5, 39.9, 44.3)
+        work += [(at, serve_kv, g + 1) for g, at in enumerate(forward)]
         for k in range(4, pieces):
             at = arrive[k]
             work.append((at, serve_x, k))
@@ -479,9 +482,7 @@
             return pltpu.make_async_copy(att.at[:, lanes], att_out.at[:, lanes], out_sem.at[5 + p])
 
         def pair(p, carry):
-            @pl.when(p % 2 == 0)
-            def _():
-                complete_kv(p // 2)
+            complete_kv(p)
 
             def between(tile):
                 for slot, action, k in work:

time: 245 us -> 242 us (0.988)
  Pallas kernels: 242 us -> 239 us
    pallas_call x1, Pallas kernels: 75.6 us -> 71.9 us  [project_and_attend(): pl.pallas_call(kernel, in_specs=[vmem, vmem, anywhere, anywhere, anywhere...]
where the time goes in v2:
time: 242 us; the launch traced here: 241 us
  Pallas kernels  239 us (99%)
    pallas_call x1, Pallas kernels, finish(): pl.pallas_call(kernel, in_specs=[anywhere] * 11 + [vmem] * 4, out_specs=[...  115 us
    pallas_call x1, Pallas kernels, project_and_attend(): pl.pallas_call(kernel, in_specs=[vmem, vmem, anywhere, anywhere, anywhere...  71.9 us
    pallas_call x1, Pallas kernels, middle(): pl.pallas_call(kernel, in_specs=[pl.BlockSpec(memory_space=pltpu.SMEM)] +...  44.8 us
    pallas_call x1, Pallas kernels, place(): pl.pallas_call(kernel, in_specs=[anywhere] * count + [vmem] * 2, out_spec...  7.65 us

profile of v2, /device:TPU:0, one launch (start us, length us, event | category | flops | bytes accessed | tf_op | source)
XLA Modules:
  0.0 240.8 jit_solution(17963489401891326439)
XLA Ops:
  1.3 71.9 %project_and_attend.1 = (bf16[8,4,192,768]{3,2,1,0:T(8,128)(2,1)}, bf16[4,4,192,768]{3,2,1,0:T(8,128)(2,1)}, bf16[768,768]{1,0:T(8,128)(2,1)}, bf16[512,768]{1,0...) custom-call(bf16[256,768]{1,0:T(8,128)(2,1)} %bitcast.22, ...), custom_call_target="tpu_custom_call" | custom-call | tf_op jit(solution)/shard_map/project_and_attend/pallas_call | solution.py:611
  73.2 44.8 %middle.1 = (bf16[256,768]{1,0:T(8,128)(2,1)}, bf16[512,768]{1,0:T(8,128)(2,1)}, f32[1,14]{1,0:T(1,128)}, bf16[9,768,768]{2,1,0:T(8,128)(2,1)}, f32[768,768]{1,0...) custom-call(s32[1,1]{1,0:T(1,128)S(6)} %copy.34.label_ref, ...), custom_call_target="tpu_custom_call" | custom-call | tf_op jit(solution)/shard_map/middle/pallas_call | solution.py:1025
  118.0 115.0 %finish.1 = (f32[256,768]{1,0:T(8,128)}, f32[512,768]{1,0:T(8,128)}, bf16[192,2304]{1,0:T(8,128)(2,1)}, bf16[192,768]{1,0:T(8,128)(2,1)}, bf16[192,3072]{1,0:T(8...) custom-call(bf16[768,768]{1,0:T(8,128)(2,1)} %get-tuple-element.64.q_h, ...), custom_call_target="tpu_custom_call" | custom-call | tf_op jit(solution)/shard_map/finish/pallas_call | solution.py:1560
  233.0 7.7 %place.1 = (f32[256,768]{1,0:T(8,128)}, f32[512,768]{1,0:T(8,128)}, f32[192,2304]{1,0:T(8,128)}, f32[192,768]{1,0:T(8,128)}, f32[192,3072]{1,0:T(8,128)}, /*inde...) custom-call(f32[256,768]{1,0:T(8,128)} %get-tuple-element.84.refs_0_, ...), custom_call_target="tpu_custom_call" | custom-call | tf_op jit(solution)/shard_map/place/pallas_call | solution.py:1651

commit v3 on v2

--- a/solution.py
+++ b/solution.py
@@ -1466,6 +1466,7 @@
             pl.when(n == 11)(lambda: stage_z(pieces))
             pl.when(n < pieces + 2)(lambda: stage_f(n - 2))
             pl.when(n == 12)(lambda: stage_f(pieces))
+            pl.when(n == 14)(stage_g)
             stage_o(n - 3)
             pl.when(n == 13)(lambda: stage_o(pieces))
             pl.when(n == 7)(cont_part)
@@ -1487,7 +1488,6 @@
                 g_copy(step).start()
 
         lax.fori_loop(pieces - 5, pieces + 3, tick, 0)
-        stage_g()
         for step in (1, 2, 3):
             slot = lax.rem(shard + step, 4)
             remote(
@@ -1600,15 +1600,18 @@
     rows, across = summed.shape[1], D // 128
 
     def kernel(*refs):
-        sources, fin, logits_in = refs[:count], refs[count], refs[count + 1]
+        sources, fin_h, logits_in = refs[:count], refs[count], refs[count + 1]
         outs = refs[count + 2 :]
         targets = outs[:count]
         o_bias, o_gain, o_in, o_stu, o_vec, o_pool, o_class, o_cb, o_logits = outs[count : count + 9]
         scratch = outs[count + 9 :]
-        held, turned, (sem_in, sem_out) = scratch[:count], scratch[count:-2], scratch[-2:]
+        held, turned, (fin, sem_in, sem_out) = scratch[:count], scratch[count:-3], scratch[-3:]
         reads = [pltpu.make_async_copy(sources[i], held[i], sem_in.at[i]) for i in order]
+        small = pltpu.make_async_copy(fin_h, fin, sem_in.at[count])
+        small.start()
         for copy in reads:
             copy.start()
+        small.wait()
 
         def side(block):
             return fin[block, :, STU:].astype(jnp.float32)
@@ -1650,7 +1653,7 @@
     vmem = pl.BlockSpec(memory_space=pltpu.VMEM)
     return pl.pallas_call(
         kernel,
-        in_specs=[anywhere] * count + [vmem] * 2,
+        in_specs=[anywhere] * (count + 1) + [vmem],
         out_specs=[anywhere] * count + [vmem] * 9,
         out_shape=[shaped(*part.shape) for part in big[:6]]
         + [jax.ShapeDtypeStruct(part.shape, part.dtype) for part in big[6:]]
@@ -1667,7 +1670,8 @@
         ],
         scratch_shapes=[pltpu.VMEM(part.shape, part.dtype) for part in big]
         + [pltpu.VMEM(part.shape, jnp.float32) for part in owned]
-        + [pltpu.SemaphoreType.DMA((count,)), pltpu.SemaphoreType.DMA((count,))],
+        + [pltpu.VMEM(summed.shape, summed.dtype)]
+        + [pltpu.SemaphoreType.DMA((count + 1,)), pltpu.SemaphoreType.DMA((count,))],
         compiler_params=pltpu.CompilerParams(vmem_limit_bytes=VMEM_ALL),
         name="place",
     )(*big, summed, logits)

time: 242 us -> 242 us (level)
  no operation moved by 1% of the time
where the time goes in v3:
time: 242 us; the launch traced here: 240 us
  Pallas kernels  238 us (98%)
    pallas_call x1, Pallas kernels, finish(): pl.pallas_call(kernel, in_specs=[anywhere] * 11 + [vmem] * 4, out_specs=[...  114 us
    pallas_call x1, Pallas kernels, project_and_attend(): pl.pallas_call(kernel, in_specs=[vmem, vmem, anywhere, anywhere, anywhere...  71.9 us
    pallas_call x1, Pallas kernels, middle(): pl.pallas_call(kernel, in_specs=[pl.BlockSpec(memory_space=pltpu.SMEM)] +...  44.8 us
    pallas_call x1, Pallas kernels, place(): pl.pallas_call(kernel, in_specs=[anywhere] * (count + 1) + [vmem], out_sp...  7.37 us

profile of v3, /device:TPU:0, one launch (start us, length us, event | category | flops | bytes accessed | tf_op | source)
XLA Modules:
  0.0 240.0 jit_solution(12305568358152747004)
XLA Ops:
  1.3 71.9 %project_and_attend.1 = (bf16[8,4,192,768]{3,2,1,0:T(8,128)(2,1)}, bf16[4,4,192,768]{3,2,1,0:T(8,128)(2,1)}, bf16[768,768]{1,0:T(8,128)(2,1)}, bf16[512,768]{1,0...) custom-call(bf16[256,768]{1,0:T(8,128)(2,1)} %bitcast.22, ...), custom_call_target="tpu_custom_call" | custom-call | tf_op jit(solution)/shard_map/project_and_attend/pallas_call | solution.py:611
  73.2 44.8 %middle.1 = (bf16[256,768]{1,0:T(8,128)(2,1)}, bf16[512,768]{1,0:T(8,128)(2,1)}, f32[1,14]{1,0:T(1,128)}, bf16[9,768,768]{2,1,0:T(8,128)(2,1)}, f32[768,768]{1,0...) custom-call(s32[1,1]{1,0:T(1,128)S(6)} %copy.34.label_ref, ...), custom_call_target="tpu_custom_call" | custom-call | tf_op jit(solution)/shard_map/middle/pallas_call | solution.py:1025
  118.0 114.4 %finish.1 = (f32[256,768]{1,0:T(8,128)}, f32[512,768]{1,0:T(8,128)}, bf16[192,2304]{1,0:T(8,128)(2,1)}, bf16[192,768]{1,0:T(8,128)(2,1)}, bf16[192,3072]{1,0:T(8...) custom-call(bf16[768,768]{1,0:T(8,128)(2,1)} %get-tuple-element.64.q_h, ...), custom_call_target="tpu_custom_call" | custom-call | tf_op jit(solution)/shard_map/finish/pallas_call | solution.py:1560
  232.4 7.4 %place.1 = (f32[256,768]{1,0:T(8,128)}, f32[512,768]{1,0:T(8,128)}, f32[192,2304]{1,0:T(8,128)}, f32[192,768]{1,0:T(8,128)}, f32[192,3072]{1,0:T(8,128)}, /*inde...) custom-call(f32[256,768]{1,0:T(8,128)} %get-tuple-element.84.refs_0_, ...), custom_call_target="tpu_custom_call" | custom-call | tf_op jit(solution)/shard_map/place/pallas_call | solution.py:1654
